TPU v7x, 32 devices: a whole 2x2x4 slice. The times are simulated.
32 devices in a mesh: phi: 16 (over z, x, core), eta: 2 (over y).
Axes of the slice: x: 2, y: 2, z: 4, core: 2. Of those that a mesh axis runs over, the one named last changes fastest.
Arguments:
- features: bfloat16 [32, 256, 256], P(None, 'phi', 'eta'), may hold values from -6 to 6
- cotangent: bfloat16 [32, 256, 256], P(None, 'phi', 'eta'), may hold values from -6 to 6
- kernel_a: bfloat16 [27, 32, 32], replicated, may hold values from -0.21875 to 0.21875
- kernel_b: bfloat16 [27, 64, 32], replicated, may hold values from -0.21875 to 0.21875
- mixing: bfloat16 [32, 64], replicated, may hold values from -0.75 to 0.75
Outputs:
- output: bfloat16 [32, 256, 256], P(None, 'phi', 'eta')
- grad_input: bfloat16 [32, 256, 256], P(None, 'phi', 'eta')
- grad_kernel_a: float32 [27, 32, 32], replicated
- grad_kernel_b: float32 [27, 64, 32], replicated
- grad_mixing: float32 [32, 64], replicated
All inputs are finite; a program needn't handle non-finite values.
Results may differ from a plain program's by a relative error of at most 0.012.
Values may be sent and summed in bfloat16 or wider, within the bound.
No kernel may reach another device: no remote copies, remote signals or barrier semaphores. Data moves between devices by JAX's collectives and lax.ppermute only.
A program may use at most 128 MiB of HBM per device.

v0:
```python
import functools
import math

import jax
import jax.numpy as jnp
from jax import lax
from jax.experimental import pallas as pl
from jax.experimental.pallas import tpu as pltpu
from jax.sharding import PartitionSpec as P


LAYERS = 32
PB = 4
BF = jnp.bfloat16
F32 = jnp.float32


def iota(shape, dim):
    return lax.broadcasted_iota(jnp.int32, shape, dim)


def dot(a, b):
    return jnp.dot(a, b, preferred_element_type=F32)


def dot_rows(a, b):
    return lax.dot_general(a, b, (((0,), (0,)), ((), ())), preferred_element_type=F32)


def fetch(sources, places, sems):
    moves = [pltpu.make_async_copy(src, dst, sems.at[i]) for i, (src, dst) in enumerate(zip(sources, places))]
    for move in moves:
        move.start()
    return moves


def pre_kernel(paired, f_hbm, c_hbm, f_own, c_own, first, second, *rest):
    f_ref, c_ref, sems = rest[-3:]
    nb = f_own.shape[0]
    moves = fetch((f_hbm, c_hbm), (f_ref, c_ref), sems)
    for move, ref, own in zip(moves, (f_ref, c_ref), (f_own, c_own)):
        move.wait()
        ch, _, cells = ref.shape
        swapped = jnp.swapaxes(ref[...].astype(F32), 0, 1)
        for j in range(nb):
            own[j] = swapped[PB * j : PB * (j + 1)].reshape(PB * ch, cells).T.astype(BF)
    e = lax.axis_index("eta") if paired else 1
    for rim, low in ((first, e), (second, 1 - e)):
        for j in range(2):
            rim[j] = f_own[(nb - 2) * (1 - low) + j]
        rim[2] = c_own[(nb - 1) * (1 - low)]
    if paired:
        partner = rest[0]
        for j in range(partner.shape[0]):
            partner[j] = c_own[(1 - e) * (nb // 2 - 1) + j]


def copies(size, times):
    shape = (size, size * times)
    return jnp.where(iota(shape, 0) == iota(shape, 1) % size, 1.0, 0.0).astype(BF)


def weights_kernel(
    ka_hbm, kbt_hbm, mix_hbm, wa, waf, wb, wbf, mp, mt, pool, up, ta, taf, tb, tbf, ka, kbt, mix, sems
):
    for move in fetch((ka_hbm, kbt_hbm, mix_hbm), (ka, kbt, mix), sems):
        move.wait()
    c1 = ka.shape[1]
    c2 = kbt.shape[2]
    width = PB * c1
    wide = PB * c2

    def flat(block):
        return block.reshape(-1, block.shape[2])

    def turned(ref):
        return jnp.swapaxes(ref[...].astype(F32), 1, 2).astype(BF)

    few = copies(c1, PB)
    many = copies(c2, PB)
    ta[...] = dot(flat(turned(ka)), few)
    taf[...] = dot(flat(ka[...]), few)
    tb[...] = dot(flat(kbt[...]), many)
    tbf[...] = dot(flat(turned(kbt)), few)

    def toeplitz(out, source, order, rows_per, cols_per, row_blocks):
        height = len(row_blocks) * rows_per
        across = PB * cols_per
        place = iota((rows_per, across), 1) // cols_per
        for b in range(3):
            for c in range(3):
                for at, q in enumerate(row_blocks):
                    value = jnp.zeros((rows_per, across), F32)
                    for a in range(3):
                        if 0 <= q + 1 - a < PB:
                            t = order(9 * a + 3 * b + c) * rows_per
                            value = jnp.where(place == q + 1 - a, source[t : t + rows_per], value)
                    first = b * height + at * rows_per
                    out[first : first + rows_per, c * across : (c + 1) * across] = value.astype(BF)

    ring = (0, 1, 2, 3, 4, 100, 100, -1)
    toeplitz(wa, ta, lambda t: t, c1, c1, ring)
    toeplitz(wb, tb, lambda t: t, c1, c2, ring)
    toeplitz(wbf, tbf, lambda t: 26 - t, c2, c1, (0, 1, 2, 3, 4, -1))
    toeplitz(waf, taf, lambda t: 26 - t, c1, c1, ring)
    mixing = mix[...]
    spread = dot(mixing, many)
    spread_t = dot(mixing.astype(F32).T.astype(BF), few)
    for p in range(PB):
        inside = iota((c1, wide), 1) // c2 == p
        mt[p * c1 : (p + 1) * c1] = jnp.where(inside, spread, 0.0).astype(BF)
        inside = iota((c2, width), 1) // c1 == p
        mp[p * c2 : (p + 1) * c2] = jnp.where(inside, spread_t, 0.0).astype(BF)
    r = iota(pool.shape, 0)
    l = iota(pool.shape, 1)
    hit = (r % c1 == l % c1) & (r // (2 * width) * 2 + r % width // c1 // 2 == l // c1)
    pool[...] = jnp.where(hit, 1.0, 0.0).astype(BF)
    r = iota(up.shape, 0)
    l = iota(up.shape, 1)
    hit = (r % c1 == l % c1) & (l // width * 2 + l % width // c1 // 2 == r // c1)
    up[...] = jnp.where(hit, 1.0, 0.0).astype(BF)


def combine(summed, width):
    rows = summed.shape[0]
    layer = iota((rows, width), 0) % LAYERS
    below = pltpu.roll(summed[:, :width], 1, 0)
    above = pltpu.roll(summed[:, 2 * width :], rows - 1, 0)
    return (
        summed[:, width : 2 * width]
        + jnp.where(layer == 0, 0.0, below)
        + jnp.where(layer == LAYERS - 1, 0.0, above)
    )


def layer_shifts(block):
    rows, width = block.shape
    layer = iota((rows, width), 0) % LAYERS
    wide = block.astype(F32)
    first = jnp.where(layer == LAYERS - 1, 0.0, pltpu.roll(wide, rows - 1, 0))
    last = jnp.where(layer == 0, 0.0, pltpu.roll(wide, 1, 0))
    return jnp.concatenate([first.astype(BF), block, last.astype(BF)], axis=1)


def taps(ref, j, start, rows):
    parts = []
    for b in range(3):
        at = start + b * LAYERS
        if not isinstance(at, int):
            at = pl.multiple_of(at, LAYERS)
        parts.append(ref[j, pl.ds(at, rows), :])
    return jnp.concatenate(parts, axis=1)


def every_other(block, which):
    count = block.shape[0] // (2 * LAYERS)
    return [block[(2 * i + which) * LAYERS : (2 * i + which + 1) * LAYERS] for i in range(count)]


def paired_rows(first, second):
    parts = []
    for block in (first, second):
        for which in range(2):
            parts.append(jnp.concatenate(every_other(block, which), axis=0))
    return jnp.concatenate(parts, axis=1)


def widen_rows(block):
    parts = []
    for i in range(block.shape[0] // LAYERS):
        part = block[i * LAYERS : (i + 1) * LAYERS]
        parts += [part, part]
    return jnp.concatenate(parts, axis=0)


def sigmoid(v):
    return 1.0 / (1.0 + jnp.exp(-v))


def edges(ref, first, last, inner, width, split):
    lane = iota((inner, width), 1)
    at = slice(LAYERS, LAYERS + inner)
    main = ref.shape[2] - width
    for j in range(first, last):
        nxt = ref[j + 1, at, :width] if j + 1 < ref.shape[0] else jnp.zeros((inner, width), BF)
        prv = ref[j - 1, at, main - width : main] if j > 0 else jnp.zeros((inner, width), BF)
        ref[j, at, main:] = jnp.where(lane < split, nxt, prv)


def blank_rims(ref):
    pad = jnp.zeros((LAYERS, ref.shape[2]), BF)
    for j in range(ref.shape[0]):
        ref[j, :LAYERS, :] = pad
        ref[j, ref.shape[1] - LAYERS :, :] = pad


def keep_inside(meta, shards_seen, value, scale):
    if meta is None or shards_seen == 1:
        return value
    r = iota(value.shape, 0)
    inside = (r >= meta[shards_seen] // scale) & (r < meta[shards_seen + 1] // scale)
    return jnp.where(inside, value, jnp.zeros_like(value))


def forward_kernel(paired, count, *refs):
    meta = None
    if not paired:
        meta, refs = refs[0], refs[1:]
    pieces, refs = refs[:count], refs[count:]
    wa, wb, mp, pool = refs[:4]
    fz, hid, slope, cz, gat, slope_b, proj = refs[4:]
    nbx = fz.shape[0]
    nc = gat.shape[0]
    rows = hid.shape[1]
    rows_c = rows // 2
    width = hid.shape[2]
    c1 = width // PB
    wide = gat.shape[2]
    blank_rims(fz)
    blank_rims(cz)
    cells = pieces[0].shape[1]
    if paired:
        own, partner, near, far = pieces
        nb = own.shape[0]
        e = lax.axis_index("eta")
        for chunk, rim, shard in ((own, near, e), (partner, far, 1 - e)):
            at = pl.multiple_of(LAYERS + shard * cells, LAYERS)
            for j in range(nb // 2 + 2):
                fz[j + 2 * (1 - e), pl.ds(at, cells), :width] = chunk[j + e * (nb // 2 - 2)]
            for j in range(2):
                fz[e * (nbx - 2) + j, pl.ds(at, cells), :width] = rim[j]
    else:
        for s in range(count // 3):
            middle, before, after = pieces[3 * s : 3 * s + 3]
            at = pl.multiple_of(LAYERS + meta[s] * cells, LAYERS)
            for j in range(2):
                fz[j, pl.ds(at, cells), :width] = before[j]
                fz[nbx - 2 + j, pl.ds(at, cells), :width] = after[j]
            for j in range(nbx - 4):
                fz[2 + j, pl.ds(at, cells), :width] = middle[j]
    edges(fz, 0, nbx, rows, width, 3 * c1)
    for j in range(nbx):
        linear = combine(dot(taps(fz, j, 0, rows), wa[...]), width)
        logistic = sigmoid(linear)
        hid[j] = (linear * logistic).astype(BF)
        slope[j] = logistic * (1.0 + linear * (1.0 - logistic))
    for j in range(nc + 2):
        first, second = max(2 * j - 1, 0), min(2 * j, nbx - 1)
        pooled = dot(paired_rows(hid[first], hid[second]), pool[...]) * 0.25
        cz[j, LAYERS : LAYERS + rows_c, :width] = keep_inside(meta, count // 3, pooled.astype(BF), 2)
    edges(cz, 1, nc + 1, rows_c, width, 3 * c1)
    for j in range(nc):
        linear = combine(dot(taps(cz, j + 1, 0, rows_c), wb[...]), wide)
        logistic = sigmoid(linear)
        gated = (linear * logistic).astype(BF)
        gat[j] = gated
        slope_b[j] = logistic * (1.0 + linear * (1.0 - logistic))
        proj[j] = dot(gated, mp[...]).astype(BF)


def backward_kernel(paired, count, *refs):
    meta = None
    if not paired:
        meta, refs = refs[0], refs[1:]
    pieces, refs = refs[:count], refs[count:]
    fz, slope, cz, gat, slope_b, wbf, mt, pool, up = refs[:9]
    gz, pk_ref = refs[9:11]
    cot, gb, fold, acc_a, acc_b, packed = refs[11:]
    nbx = fz.shape[0]
    nb = nbx - 4
    nc = gat.shape[0]
    rows = cot.shape[1]
    rows_c = rows // 2
    width = cot.shape[2]
    wide = gat.shape[2]
    c1 = width // PB
    c2 = wide // PB
    cells = pieces[0].shape[1]
    blank_rims(gz)
    blank_rims(gb)
    if paired:
        own, partner, near, far = pieces
        e = lax.axis_index("eta")
        for rim, shard in ((near, e), (far, 1 - e)):
            at = pl.multiple_of(shard * cells, cells)
            cot[1 + e * (nbx - 3), pl.ds(at, cells), :] = rim[2]
            for j in range(partner.shape[0]):
                if rim is near:
                    block = own[j + e * (own.shape[0] // 2 - 1)]
                else:
                    block = partner[j]
                cot[j + 2 - e, pl.ds(at, cells), :] = block
        own, own_at, own_at_c = rows, 0, 0
    else:
        for s in range(count // 3):
            middle, before, after = pieces[3 * s : 3 * s + 3]
            at = pl.multiple_of(meta[s] * cells, cells)
            cot[1, pl.ds(at, cells), :] = before[2]
            cot[nbx - 2, pl.ds(at, cells), :] = after[2]
            for j in range(nb):
                cot[2 + j, pl.ds(at, cells), :] = middle[j]
        own = cells
        own_at = pl.multiple_of(meta[0] * own, own)
        own_at_c = pl.multiple_of(meta[0] * (own // 2), own // 2)
    own_c = own // 2

    for j in range(nc):
        fold[j] = dot(paired_rows(cot[2 * j + 1], cot[2 * j + 2]), pool[...]).astype(BF)
        grad = dot(fold[j], mt[...]) * slope_b[j]
        gb[j, LAYERS : LAYERS + rows_c, :wide] = keep_inside(meta, count // 3, grad.astype(BF), 2)
    edges(gb, 0, nc, rows_c, width, c2)
    for j in range(nc):
        grad = combine(dot(taps(gb, j, 0, rows_c), wbf[...]), width).astype(BF)
        spread = 0.25 * dot(grad, up[...])
        for k in range(2):
            f = 2 * j + 1 + k
            total = cot[f].astype(F32) + widen_rows(spread[:, k * width : (k + 1) * width])
            value = (total * slope[f]).astype(BF)
            gz[f, LAYERS : LAYERS + rows, :width] = keep_inside(meta, count // 3, value, 1)
    edges(gz, 2, nbx - 2, rows, width, 3 * c1)

    def own_half(value, j):
        p = iota(value.shape, 1) // (value.shape[1] // PB)
        if j == 0:
            value = jnp.where(p >= PB // 2, value, jnp.zeros_like(value))
        if j == nc - 1:
            value = jnp.where(p < PB // 2, value, jnp.zeros_like(value))
        return value

    lhs = jnp.concatenate(
        [layer_shifts(gz[2 + j, pl.ds(LAYERS + own_at, own), :width]) for j in range(nb)], axis=0
    )
    rhs = jnp.concatenate([taps(fz, 2 + j, own_at, own) for j in range(nb)], axis=0)
    acc_a[...] = dot_rows(lhs, rhs)
    lhs = jnp.concatenate(
        [layer_shifts(own_half(gb[j, pl.ds(LAYERS + own_at_c, own_c), :wide], j)) for j in range(nc)], axis=0
    )
    rhs = jnp.concatenate([taps(cz, j + 1, own_at_c, own_c) for j in range(nc)], axis=0)
    acc_b[...] = dot_rows(lhs, rhs)
    lhs = jnp.concatenate([gat[j, pl.ds(own_at_c, own_c), :] for j in range(nc)], axis=0)
    rhs = jnp.concatenate([own_half(fold[j, pl.ds(own_at_c, own_c), :], j) for j in range(nc)], axis=0)
    mixed = dot_rows(lhs, rhs)
    mix_sum = mixed[:c2, :c1]
    for p in range(1, PB):
        mix_sum = mix_sum + mixed[p * c2 : (p + 1) * c2, p * c1 : (p + 1) * c1]
    packed[c1:, 27 * c1 : 28 * c1] = mix_sum
    packed[:c1, 27 * c1 : 28 * c1] = jnp.zeros((c1, c1), F32)
    span = 2 * width
    for acc, outs, first in ((acc_a, c1, 0), (acc_b, c2, c1)):
        for b in range(3):
            for c in range(3):
                total = None
                for p in range(PB):
                    at = (c * PB + p) * outs
                    part = acc[at : at + outs, b * span : (b + 1) * span]
                    part = pltpu.roll(part, (span - (p - 1) * c1) % span, 1)
                    total = part if total is None else total + part
                for a in range(3):
                    t = 9 * a + 3 * b + c
                    packed[first : first + outs, t * c1 : (t + 1) * c1] = total[:, a * c1 : (a + 1) * c1]
    chunk = pk_ref.shape[1]
    per = packed.shape[0] // chunk
    used = packed.shape[1] // 128 * per
    for v in range(packed.shape[1] // 128):
        for r in range(per):
            pk_ref[v * per + r] = packed[r * chunk : (r + 1) * chunk, v * 128 : (v + 1) * 128].astype(BF)
    for v in range(used, pk_ref.shape[0]):
        pk_ref[v] = jnp.zeros(pk_ref.shape[1:], BF)


def finish_kernel(paired, *refs):
    meta = None
    if not paired:
        meta, refs = refs[0], refs[1:]
    gz, hid, proj, waf, up = refs[:5]
    outs = refs[5:-1]
    buf = refs[-1]
    nb = gz.shape[0] - 4
    width = hid.shape[2]
    cells = outs[0].shape[2]
    if paired:
        own, own_at, own_at_c = hid.shape[1], 0, 0
        e = lax.axis_index("eta")
        starts = [pl.multiple_of(e * cells, cells), pl.multiple_of((1 - e) * cells, cells)]
    else:
        own = cells
        own_at = pl.multiple_of(meta[0] * own, own)
        own_at_c = pl.multiple_of(meta[0] * (own // 2), own // 2)
        starts = [0]

    def write(value, place):
        buf[place] = value
        for out, start in zip(outs, starts):
            out[place] = buf[place, pl.ds(start, cells), :].T.astype(BF)

    for j in range(nb):
        grad = combine(dot(taps(gz, 2 + j, own_at, own), waf[...]), width)
        write(grad, nb + j)
    for j in range(nb):
        k = (j + 1) % 2
        spread = dot(proj[(j + 1) // 2, pl.ds(own_at_c, own // 2), :], up[:, k * width : (k + 1) * width])
        write(hid[2 + j, pl.ds(own_at, own), :].astype(F32) + widen_rows(spread), j)


def restore_kernel(kept, received, out_ref, gin_ref):
    ch, rows, cells = out_ref.shape
    half = rows // 2
    e = lax.axis_index("eta")
    for k, ref in enumerate((out_ref, gin_ref)):
        at = k * half // PB
        mine = kept[at : at + half // PB].astype(F32)
        other = received[at : at + half // PB].astype(F32)
        first = jnp.where(e == 0, mine, other).reshape(half, ch, cells)
        second = jnp.where(e == 0, other, mine).reshape(half, ch, cells)
        ref[...] = jnp.swapaxes(jnp.concatenate([first, second], axis=0), 0, 1).astype(BF)


def sum_kernel(x_ref, o_ref):
    total = jnp.sum(x_ref[...].astype(F32), axis=0).astype(BF)
    o_ref[...] = jnp.broadcast_to(total[None], o_ref.shape)


def post_kernel(factor, x_ref, ga_ref, gb_ref, gm_ref, buf):
    chunk = x_ref.shape[1]
    per = buf.shape[0] // chunk
    c1 = ga_ref.shape[1]
    for v in range(buf.shape[1] // 128):
        for r in range(per):
            buf[r * chunk : (r + 1) * chunk, v * 128 : (v + 1) * 128] = x_ref[v * per + r].astype(F32) * factor
    for t in range(27):
        ga_ref[t] = buf[:c1, t * c1 : (t + 1) * c1]
        gb_ref[t] = buf[c1:, t * c1 : (t + 1) * c1].T
    gm_ref[...] = buf[c1:, 27 * c1 : 28 * c1].T


def call(kernel, outs, *args, scratch=(), smem=0, near=(), far=()):
    args = list(args)
    specs = []
    for place in range(len(args)):
        if place < smem:
            specs.append(pl.BlockSpec(memory_space=pltpu.SMEM))
        elif place in far:
            specs.append(pl.BlockSpec(memory_space=pl.ANY))
            args[place] = pltpu.with_memory_space_constraint(args[place], pltpu.HBM)
        else:
            specs.append(pl.BlockSpec(memory_space=pltpu.VMEM))
            if place in near:
                args[place] = pltpu.with_memory_space_constraint(args[place], pltpu.VMEM)
    return pl.pallas_call(
        kernel,
        out_shape=outs,
        in_specs=specs,
        out_specs=tuple(pl.BlockSpec(memory_space=pltpu.VMEM) for _ in outs),
        scratch_shapes=list(scratch),
        compiler_params=pltpu.CompilerParams(vmem_limit_bytes=32 * 1024 * 1024),
    )(*args)


def shape(dims, dtype=BF):
    return jax.ShapeDtypeStruct(tuple(dims), dtype)


AXES = ("phi", "eta")


def moves(n_phi, n_eta, rule):
    found = []
    for p in range(n_phi):
        for s in range(n_eta):
            step, t = rule(p, s)
            if 0 <= t < n_eta:
                found.append((p * n_eta + s, (p + step) % n_phi * n_eta + t))
    return found


def gather_pair(f_own, c_own, c_sent, near, far):
    n_phi = lax.axis_size("phi")

    def send(value, rule):
        return lax.ppermute(value, AXES, moves(n_phi, 2, rule))

    far = send(far, lambda p, s: (2 * s - 1, 1 - s))
    near = send(near, lambda p, s: (1 - 2 * s, s))
    f_other = send(f_own, lambda p, s: (0, 1 - s))
    c_other = send(c_sent, lambda p, s: (0, 1 - s))
    return [f_own, f_other, near, far], [c_own, c_other, near, far]


def gather_window(f_own, c_own, low, high):
    n_phi = lax.axis_size("phi")
    n_eta = lax.axis_size("eta")
    f_pieces = []
    c_pieces = []
    for step in window_steps(n_eta):
        send = lambda value, move: lax.ppermute(value, AXES, moves(n_phi, n_eta, lambda p, s: (move, s - step)))
        rims = [send(high, 1), send(low, -1)]
        f_pieces += [f_own if step == 0 else send(f_own, 0)] + rims
        c_pieces += [c_own if step == 0 else send(c_own, 0)] + rims
    return f_pieces, c_pieces


def window_steps(n_eta):
    return [0] if n_eta == 1 else [0, -1, 1, -2, 2]


def window_meta(n_eta, cells):
    e = lax.axis_index("eta")
    steps = window_steps(n_eta)
    middle = len(steps) // 2
    values = [middle + step for step in steps]
    values += [jnp.maximum(0, middle - e) * cells, jnp.minimum(len(steps), n_eta + middle - e) * cells]
    return jnp.stack([jnp.asarray(v, jnp.int32) for v in values])


def shards(features, cotangent, kernel_a, kernel_b, mixing):
    c1, n_rows, cells = features.shape
    c2 = kernel_b.shape[1]
    nb = n_rows // PB
    width = PB * c1
    n_eta = lax.axis_size("eta")
    paired = n_eta == 2 and nb % 4 == 0
    block = (cells, width)
    f_own, c_own, first, second, *c_sent = call(
        functools.partial(pre_kernel, paired),
        tuple(shape((n,) + block) for n in (nb, nb, 3, 3) + ((nb // 2 + 1,) if paired else ())),
        features,
        cotangent,
        scratch=(
            pltpu.VMEM(features.shape, BF),
            pltpu.VMEM(features.shape, BF),
            pltpu.SemaphoreType.DMA((2,)),
        ),
        far=(0, 1),
    )
    if paired:
        f_pieces, c_pieces = gather_pair(f_own, c_own, c_sent[0], first, second)
        meta = []
        nbx = nb // 2 + 4
        rows = 2 * cells
    else:
        f_pieces, c_pieces = gather_window(f_own, c_own, first, second)
        meta = [window_meta(n_eta, cells)]
        nbx = nb + 4
        rows = len(window_steps(n_eta)) * cells
    wa, waf, wb, wbf, mp, mt, pool, up = call(
        weights_kernel,
        (
            pltpu.VMEM((3 * 2 * width, 3 * width), BF),
            pltpu.VMEM((3 * 2 * width, 3 * width), BF),
            pltpu.VMEM((3 * 2 * width, 3 * PB * c2), BF),
            pltpu.VMEM((3 * 6 * c2, 3 * width), BF),
            pltpu.VMEM((PB * c2, width), BF),
            pltpu.VMEM((width, PB * c2), BF),
            pltpu.VMEM((4 * width, width), BF),
            pltpu.VMEM((width, 2 * width), BF),
        ),
        kernel_a,
        jnp.swapaxes(kernel_b, 1, 2),
        mixing,
        scratch=(
            pltpu.VMEM((27 * c1, width), F32),
            pltpu.VMEM((27 * c1, width), F32),
            pltpu.VMEM((27 * c1, PB * c2), F32),
            pltpu.VMEM((27 * c2, width), F32),
            pltpu.VMEM(kernel_a.shape, BF),
            pltpu.VMEM((27, c1, c2), BF),
            pltpu.VMEM(mixing.shape, BF),
            pltpu.SemaphoreType.DMA((3,)),
        ),
        far=(0, 1, 2),
    )
    nc = nbx // 2 - 1
    rows_c = rows // 2
    devices = lax.axis_size("phi") * n_eta
    lanes = 28 * c1
    total_rows = (c1 + c2) * lanes // 128
    chunk = next(d for d in range(8, c1 + c2 + 1, 8) if (c1 + c2) % d == 0 and total_rows <= d * devices)
    tall = rows + 2 * LAYERS
    tall_c = rows_c + 2 * LAYERS
    skip = len(meta)
    count = len(f_pieces)
    matrices = (wa, wb, mp, pool)
    fz, hid, slope, cz, gat, slope_b, proj = call(
        functools.partial(forward_kernel, paired, count),
        (
            pltpu.VMEM((nbx, tall, 2 * width), BF),
            pltpu.VMEM((nbx, rows, width), BF),
            pltpu.VMEM((nbx, rows, width), F32),
            pltpu.VMEM((nc + 2, tall_c, 2 * width), BF),
            pltpu.VMEM((nc, rows_c, PB * c2), BF),
            pltpu.VMEM((nc, rows_c, PB * c2), F32),
            pltpu.VMEM((nc, rows_c, width), BF),
        ),
        *meta,
        *f_pieces,
        *matrices,
        smem=skip,
        near=range(skip + 1, skip + count + len(matrices)),
    )
    inner = (fz, slope, cz, gat, slope_b, wbf, mt, pool, up)
    gz, terms = call(
        functools.partial(backward_kernel, paired, count),
        (pltpu.VMEM((nbx, tall, 2 * width), BF), shape((devices, chunk, 128))),
        *meta,
        *c_pieces,
        *inner,
        scratch=(
            pltpu.VMEM((nbx, rows, width), BF),
            pltpu.VMEM((nc, tall_c, PB * c2 + width), BF),
            pltpu.VMEM((nc, rows_c, width), BF),
            pltpu.VMEM((3 * width, 6 * width), F32),
            pltpu.VMEM((3 * PB * c2, 6 * width), F32),
            pltpu.VMEM((c1 + c2, lanes), F32),
        ),
        smem=skip,
        near=range(skip + 1, skip + count + len(inner)),
    )
    terms = lax.all_to_all(terms, AXES, 0, 0, tiled=True)
    blocks = 2 * (nbx - 4)
    results = call(
        functools.partial(finish_kernel, paired),
        (shape((blocks, width, cells)),) * (2 if paired else 1),
        *meta,
        gz,
        hid,
        proj,
        waf,
        up,
        scratch=(pltpu.VMEM((blocks, rows if paired else cells, width), F32),),
        smem=skip,
        near=range(skip, skip + 5),
    )
    if paired:
        kept, sent = results
        received = lax.ppermute(sent, AXES, moves(lax.axis_size("phi"), 2, lambda p, s: (0, 1 - s)))
        terms, kept = lax.optimization_barrier((terms, kept))
        output, grad_input = call(restore_kernel, (shape(features.shape), shape(features.shape)), kept, received)
    else:
        output, grad_input = (
            jnp.transpose(part.reshape(n_rows, c1, cells), (1, 0, 2)) for part in (results[0][:nb], results[0][nb:])
        )
    (sums,) = call(sum_kernel, (shape(terms.shape),), terms)
    sums = lax.all_to_all(sums, AXES, 0, 0, tiled=True)
    cell_count = n_rows * cells * devices
    grad_a, grad_b, grad_mix = call(
        functools.partial(post_kernel, 1.0 / math.sqrt(cell_count)),
        (shape((27, c1, c1), F32), shape((27, c1, c2), F32), shape((c1, c2), F32)),
        sums,
        scratch=(pltpu.VMEM((c1 + c2, lanes), F32),),
    )
    return output, grad_input, grad_a, jnp.swapaxes(grad_b, 1, 2), grad_mix


def solution(mesh):
    in_specs = (P(None, "phi", "eta"), P(None, "phi", "eta"), P(), P(), P())
    out_specs = (P(None, "phi", "eta"), P(None, "phi", "eta"), P(), P(), P())

    return jax.shard_map(shards, mesh=mesh, in_specs=in_specs, out_specs=out_specs, check_vma=False)
```

profile of v0, /device:TPU:0, one launch (start us, length us, event | category | flops | bytes accessed | tf_op | source)
XLA Modules:
  0.0 47.1 jit_solution(1414428620688099749)
XLA Ops:
  0.6 1.2 %shard_map.92 = (bf16[4,128,128]{2,1,0:T(8,128)(2,1)S(1)}, bf16[4,128,128]{2,1,0:T(8,128)(2,1)S(1)}, bf16[3,128,128]{2,1,0:T(8,128)(2,1)S(1)}, bf16[3,128,128]{2,1,0:T(8,128)(2,1)S(1)}, bf16[3,128,128]{2,1,0:T(8,128)(2,1)S(1)}) custom-call(bf16[32,16,128]{2,1,0:T(8,128)(2,1)} %f_hbm.1, bf16[32,16,128]{2,1,0:T(8,128)(2,1)} %c_hbm.1), custom_call_target="tpu_custom_call" | custom-call | tf_op jit(solution)/shard_map/pallas_call | solution.py:449
  1.9 3.1 %collective-permute-start.3 = (bf16[4,128,128]{2,1,0:T(8,128)(2,1)S(1)}, bf16[4,128,128]{2,1,0:T(8,128)(2,1)S(1)}, u32[]{:S(2)}, u32[]{:S(2)}) collective-permute-start(bf16[4,128,128]{2,1,0:T(8,128)(2,1)S(1)} %get-tuple-element.40.refs_0_), channel_id=1, source_target_pairs={{0,1},{1,0},{2,3},{3,2},{4,5},{5,4},{6,7},{7,6},{8,9},{9,8},{10,11... | collective-permute-start | bytes 393224 | tf_op jit(solution)/shard_map/ppermute | solution.py:480
  4.9 0.0 collective-permute-start.1
  4.9 4.6 %collective-permute-start.2 = (bf16[3,128,128]{2,1,0:T(8,128)(2,1)S(1)}, bf16[3,128,128]{2,1,0:T(8,128)(2,1)S(1)}, u32[]{:S(2)}, u32[]{:S(2)}) collective-permute-start(bf16[3,128,128]{2,1,0:T(8,128)(2,1)S(1)} %get-tuple-element.39), channel_id=1, source_target_pairs={{0,31},{1,2},{2,1},{3,4},{4,3},{5,6},{6,5},{7,8},{8,7},{9,10},{10,... | collective-permute-start | bytes 294920 | tf_op jit(solution)/shard_map/ppermute | solution.py:480
  9.5 0.0 collective-permute-start
  9.5 2.0 %shard_map.93 = (bf16[768,384]{1,0:T(8,128)(2,1)S(1)}, bf16[768,384]{1,0:T(8,128)(2,1)S(1)}, bf16[768,768]{1,0:T(8,128)(2,1)S(1)}, bf16[1152,384]{1,0:T(8,128)(2...) custom-call(bf16[27,32,32]{2,1,0:T(8,128)(2,1)} %ka_hbm.1, ...), custom_call_target="tpu_custom_call" | custom-call | tf_op jit(solution)/shard_map/pallas_call | solution.py:449
  11.6 0.1 collective-permute-done.1.refs_2_
  11.7 1.0 %collective-permute-done.2.refs_3_ = bf16[3,128,128]{2,1,0:T(8,128)(2,1)S(1)} collective-permute-done((bf16[3,128,128]{2,1,0:T(8,128)(2,1)S(1)}, bf16[3,128,128]{2,1,0:T(8,128)(2,1)S(1)}, u32[]{:S(2)}, u32[]{:S(2)}) %collective-permute-start.2) | collective-permute-done | bytes 98336 | tf_op jit(solution)/shard_map/ppermute | solution.py:480
  12.7 0.0 collective-permute-done.3.refs_1_
  12.7 2.4 %shard_map.94 = (bf16[6,320,256]{2,1,0:T(8,128)(2,1)S(1)}, bf16[6,256,128]{2,1,0:T(8,128)(2,1)S(1)}, f32[6,256,128]{2,1,0:T(8,128)S(1)}, bf16[4,192,256]{2,1,0:T...) custom-call(bf16[4,128,128]{2,1,0:T(8,128)(2,1)S(1)} %get-tuple-elem, ...), custom_call_target="tpu_custom_call" | custom-call | tf_op jit(solution)/shard_map/pallas_call | solution.py:449
  15.1 0.0 collective-permute-done.refs_1_
  15.2 3.1 %shard_map.95 = (bf16[6,320,256]{2,1,0:T(8,128)(2,1)S(1)}, bf16[32,24,128]{2,1,0:T(8,128)(2,1)}) custom-call(bf16[4,128,128]{2,1,0:T(8,128)(2,1)S(1)} %get-tuple-element.36.refs_0_, bf16[3,128,128]{2,1,0:T(8,128)(2,1)S(1)} %collective-permute-done.refs_1_, bf16[3,128,128]{2,1,0:T(8,128)(2,1)S(1)} %collective-permute-done.1.refs_2_, ...), custom_call_target="tpu_custom_call" | custom-call | tf_op jit(solution)/shard_map/pallas_call | solution.py:449
  18.2 4.9 %all-to-all-start = ((bf16[32,24,128]{2,1,0:T(8,128)(2,1)}), bf16[32,24,128]{2,1,0:T(8,128)(2,1)S(1)}, u32[]{:S(2)}, u32[]{:S(2)}) async-start(bf16[32,24,128]{2,1,0:T(8,128)(2,1)} %get-tuple-element.53), calls=%async_computation | async-start | bytes 393216 | tf_op jit(solution)/shard_map/all_to_all | solution.py:618
  23.2 0.7 %shard_map.96 = (bf16[4,128,128]{2,1,0:T(8,128)(2,1)S(1)}, bf16[4,128,128]{2,1,0:T(8,128)(2,1)S(1)}) custom-call(bf16[6,320,256]{2,1,0:T(8,128)(2,1)S(1)} %get-tuple-element.54.refs_0_, bf16[6,256,128]{2,1,0:T(8,128)(2,1)S(1)} %get-tuple-element.55.refs_1_, bf16[2,128,128]{2,1,0:T(8,128)(2,1)S(1)} %get-tuple-element.56.refs_2_, ...), custom_call_target="tpu_custom_call" | custom-call | tf_op jit(solution)/shard_map/pallas_call | solution.py:449
  23.9 8.9 %all-to-all-done.x_ref = bf16[32,24,128]{2,1,0:T(8,128)(2,1)S(1)} async-done(((bf16[32,24,128]{2,1,0:T(8,128)(2,1)}), bf16[32,24,128]{2,1,0:T(8,128)(2,1)S(1)}, u32[]{:S(2)}, u32[]{:S(2)}) %all-to-all-start) | async-done | bytes 196640 | tf_op jit(solution)/shard_map/all_to_all | solution.py:618
  32.8 0.7 %shard_map.98 = bf16[32,24,128]{2,1,0:T(8,128)(2,1)} custom-call(bf16[32,24,128]{2,1,0:T(8,128)(2,1)S(1)} %all-to-all-done.x_ref), custom_call_target="tpu_custom_call" | custom-call | tf_op jit(solution)/shard_map/pallas_call | solution.py:449
  33.5 2.6 %all-to-all-start.1 = ((bf16[32,24,128]{2,1,0:T(8,128)(2,1)}), bf16[32,24,128]{2,1,0:T(8,128)(2,1)S(1)}, u32[]{:S(2)}, u32[]{:S(2)}) async-start(bf16[32,24,128]{2,1,0:T(8,128)(2,1)} %shard_map.98), calls=%async_computation.1 | async-start | bytes 393216 | tf_op jit(solution)/shard_map/all_to_all | solution.py:643
  36.1 1.7 %collective-permute-start.4 = (bf16[4,128,128]{2,1,0:T(8,128)(2,1)S(1)}, bf16[4,128,128]{2,1,0:T(8,128)(2,1)S(1)}, u32[]{:S(2)}, u32[]{:S(2)}) collective-permute-start(bf16[4,128,128]{2,1,0:T(8,128)(2,1)S(1)} %get-tuple-element.60), channel_id=1, source_target_pairs={{0,1},{1,0},{2,3},{3,2},{4,5},{5,4},{6,7},{7,6},{8,9},{9,8},{10,11... | collective-permute-start | bytes 393224 | tf_op jit(solution)/shard_map/ppermute | solution.py:635
  37.9 5.5 %collective-permute-done.4.received = bf16[4,128,128]{2,1,0:T(8,128)(2,1)S(1)} collective-permute-done((bf16[4,128,128]{2,1,0:T(8,128)(2,1)S(1)}, bf16[4,128,128]{2,1,0:T(8,128)(2,1)S(1)}, u32[]{:S(2)}, u32[]{:S(2)}) %collective-permute-start.4) | collective-permute-done | bytes 131104 | tf_op jit(solution)/shard_map/ppermute | solution.py:635
  43.3 0.8 %shard_map.97 = (bf16[32,16,128]{2,1,0:T(8,128)(2,1)}, bf16[32,16,128]{2,1,0:T(8,128)(2,1)}) custom-call(bf16[4,128,128]{2,1,0:T(8,128)(2,1)S(1)} %get-tuple-element.59.kept, bf16[4,128,128]{2,1,0:T(8,128)(2,1)S(1)} %collective-permute-done.4.received), custom_call_target="tpu_custom_call" | custom-call | tf_op jit(solution)/shard_map/pallas_call | solution.py:449
  44.1 1.7 %all-to-all-done.1.x_ref = bf16[32,24,128]{2,1,0:T(8,128)(2,1)S(1)} async-done(((bf16[32,24,128]{2,1,0:T(8,128)(2,1)}), bf16[32,24,128]{2,1,0:T(8,128)(2,1)S(1)}, u32[]{:S(2)}, u32[]{:S(2)}) %all-to-all-start.1) | async-done | bytes 196640 | tf_op jit(solution)/shard_map/all_to_all | solution.py:643
  45.8 1.4 %shard_map.99 = (f32[27,32,32]{2,1,0:T(8,128)}, f32[27,32,64]{2,1,0:T(8,128)}, f32[32,64]{1,0:T(8,128)}) custom-call(bf16[32,24,128]{2,1,0:T(8,128)(2,1)S(1)} %all-to-all-done.1.x_ref), custom_call_target="tpu_custom_call" | custom-call | tf_op jit(solution)/shard_map/pallas_call | solution.py:449
Async XLA Ops:
  1.9 10.8 %collective-permute-start.3 = (bf16[4,128,128]{2,1,0:T(8,128)(2,1)S(1)}, bf16[4,128,128]{2,1,0:T(8,128)(2,1)S(1)}, u32[]{:S(2)}, u32[]{:S(2)}) collective-permute-start(bf16[4,128,128]{2,1,0:T(8,128)(2,1)S(1)} %get-tuple-element.40.refs_0_), channel_id=1, source_target_pairs={{0,1},{1,0},{2,3},{3,2},{4,5},{5,4},{6,7},{7,6},{8,9},{9,8},{10,11... | collective-permute-start | bytes 393224 | tf_op jit(solution)/shard_map/ppermute | solution.py:480
  4.9 6.7 %collective-permute-start.1 = (bf16[3,128,128]{2,1,0:T(8,128)(2,1)S(1)}, bf16[3,128,128]{2,1,0:T(8,128)(2,1)S(1)}, u32[]{:S(2)}, u32[]{:S(2)}) collective-permute-start(bf16[3,128,128]{2,1,0:T(8,128)(2,1)S(1)} %get-tuple-element.38), channel_id=1, source_target_pairs={{0,2},{1,31},{2,4},{3,1},{4,6},{5,3},{6,8},{7,5},{8,10},{9,7},{10,... | collective-permute-start | bytes 294920 | tf_op jit(solution)/shard_map/ppermute | solution.py:480
  4.9 7.7 %collective-permute-start.2 = (bf16[3,128,128]{2,1,0:T(8,128)(2,1)S(1)}, bf16[3,128,128]{2,1,0:T(8,128)(2,1)S(1)}, u32[]{:S(2)}, u32[]{:S(2)}) collective-permute-start(bf16[3,128,128]{2,1,0:T(8,128)(2,1)S(1)} %get-tuple-element.39), channel_id=1, source_target_pairs={{0,31},{1,2},{2,1},{3,4},{4,3},{5,6},{6,5},{7,8},{8,7},{9,10},{10,... | collective-permute-start | bytes 294920 | tf_op jit(solution)/shard_map/ppermute | solution.py:480
  9.5 5.6 %collective-permute-start = (bf16[3,128,128]{2,1,0:T(8,128)(2,1)S(1)}, bf16[3,128,128]{2,1,0:T(8,128)(2,1)S(1)}, u32[]{:S(2)}, u32[]{:S(2)}) collective-permute-start(bf16[3,128,128]{2,1,0:T(8,128)(2,1)S(1)} %get-tuple-element.37), channel_id=1, source_target_pairs={{0,1},{1,0},{2,3},{3,2},{4,5},{5,4},{6,7},{7,6},{8,9},{9,8},{10,11... | collective-permute-start | bytes 294920 | tf_op jit(solution)/shard_map/ppermute | solution.py:480
  18.2 14.6 %all-to-all-start = ((bf16[32,24,128]{2,1,0:T(8,128)(2,1)}), bf16[32,24,128]{2,1,0:T(8,128)(2,1)S(1)}, u32[]{:S(2)}, u32[]{:S(2)}) async-start(bf16[32,24,128]{2,1,0:T(8,128)(2,1)} %get-tuple-element.53), calls=%async_computation | async-start | bytes 393216 | tf_op jit(solution)/shard_map/all_to_all | solution.py:618
  33.5 12.2 %all-to-all-start.1 = ((bf16[32,24,128]{2,1,0:T(8,128)(2,1)}), bf16[32,24,128]{2,1,0:T(8,128)(2,1)S(1)}, u32[]{:S(2)}, u32[]{:S(2)}) async-start(bf16[32,24,128]{2,1,0:T(8,128)(2,1)} %shard_map.98), calls=%async_computation.1 | async-start | bytes 393216 | tf_op jit(solution)/shard_map/all_to_all | solution.py:643
  36.1 7.2 %collective-permute-start.4 = (bf16[4,128,128]{2,1,0:T(8,128)(2,1)S(1)}, bf16[4,128,128]{2,1,0:T(8,128)(2,1)S(1)}, u32[]{:S(2)}, u32[]{:S(2)}) collective-permute-start(bf16[4,128,128]{2,1,0:T(8,128)(2,1)S(1)} %get-tuple-element.60), channel_id=1, source_target_pairs={{0,1},{1,0},{2,3},{3,2},{4,5},{5,4},{6,7},{7,6},{8,9},{9,8},{10,11... | collective-permute-start | bytes 393224 | tf_op jit(solution)/shard_map/ppermute | solution.py:635
where the time goes:
time: 47.4 us; the launch traced here: 47.1 us
  waiting for transfers between devices  17.1 us (36%)
  starting transfers between devices  16.9 us (36%)
  Pallas kernels  12.4 us (26%)
  between operations  0.69 us (1%)
    pallas_call x8, Pallas kernels, call(): pl.pallas_call(kernel, out_shape=outs, in_specs=specs, out_specs=tuple((p...  12.4 us
    all_to_all x1, waiting for transfers between devices, shards(): terms = lax.all_to_all(terms, AXES, 0, 0, tiled=True)  8.89 us
    ppermute x4, starting transfers between devices, send(): return lax.ppermute(value, AXES, moves(n_phi, 2, rule))  7.65 us
    ppermute x1, waiting for transfers between devices, shards(): lax.ppermute(sent, AXES, moves(lax.axis_size('phi'), 2, lambda p, s: (0,...  5.46 us
    all_to_all x1, starting transfers between devices, shards(): terms = lax.all_to_all(terms, AXES, 0, 0, tiled=True)  4.95 us
    all_to_all x1, starting transfers between devices, shards(): sums = lax.all_to_all(sums, AXES, 0, 0, tiled=True)  2.58 us
    ppermute x1, starting transfers between devices, shards(): lax.ppermute(sent, AXES, moves(lax.axis_size('phi'), 2, lambda p, s: (0,...  1.72 us
    all_to_all x1, waiting for transfers between devices, shards(): sums = lax.all_to_all(sums, AXES, 0, 0, tiled=True)  1.66 us
  transfers between devices with their start and end apart: 7, of which 5 were waited for; matrix products, arithmetic and copies ran while one was open for 0% of the time, Pallas kernels for 13%

commit v1 on v0

--- a/solution.py
+++ b/solution.py
@@ -202,11 +202,46 @@
     return jnp.where(inside, value, jnp.zeros_like(value))
 
 
+def clamped_edges(ref, j, inner, width, split):
+    lane = iota((inner, width), 1)
+    at = slice(LAYERS, LAYERS + inner)
+    nxt = ref[jnp.minimum(j + 1, ref.shape[0] - 1), at, :width]
+    prv = ref[jnp.maximum(j - 1, 0), at, :width]
+    ref[j, at, width:] = jnp.where(lane < split, nxt, prv)
+
+
+def forward_block(j, fz, hid, slope, wa):
+    rows, width = hid.shape[1:]
+    linear = combine(dot(taps(fz, j, 0, rows), wa[...]), width)
+    logistic = sigmoid(linear)
+    hid[j] = (linear * logistic).astype(BF)
+    slope[j] = logistic * (1.0 + linear * (1.0 - logistic))
+
+
+def chunk_kernel(own, partner, wa, fz, hid, slope):
+    nbx = fz.shape[0]
+    nb, cells, width = own.shape
+    rows = hid.shape[1]
+    e = lax.axis_index("eta")
+    blank_rims(fz)
+    for chunk, shard in ((own, e), (partner, 1 - e)):
+        at = pl.multiple_of(LAYERS + shard * cells, LAYERS)
+        for j in range(nb // 2 + 2):
+            fz[j + 2 * (1 - e), pl.ds(at, cells), :width] = chunk[j + e * (nb // 2 - 2)]
+    first = 3 * (1 - e)
+    for j in range(nbx - 3):
+        clamped_edges(fz, first + j, rows, width, 3 * width // PB)
+    for j in range(nbx - 3):
+        forward_block(first + j, fz, hid, slope, wa)
+
+
 def forward_kernel(paired, count, *refs):
     meta = None
     if not paired:
         meta, refs = refs[0], refs[1:]
     pieces, refs = refs[:count], refs[count:]
+    if paired:
+        refs = refs[3:]
     wa, wb, mp, pool = refs[:4]
     fz, hid, slope, cz, gat, slope_b, proj = refs[4:]
     nbx = fz.shape[0]
@@ -216,20 +251,22 @@
     width = hid.shape[2]
     c1 = width // PB
     wide = gat.shape[2]
-    blank_rims(fz)
     blank_rims(cz)
     cells = pieces[0].shape[1]
     if paired:
-        own, partner, near, far = pieces
-        nb = own.shape[0]
+        near, far = pieces
         e = lax.axis_index("eta")
-        for chunk, rim, shard in ((own, near, e), (partner, far, 1 - e)):
+        for rim, shard in ((near, e), (far, 1 - e)):
             at = pl.multiple_of(LAYERS + shard * cells, LAYERS)
-            for j in range(nb // 2 + 2):
-                fz[j + 2 * (1 - e), pl.ds(at, cells), :width] = chunk[j + e * (nb // 2 - 2)]
             for j in range(2):
                 fz[e * (nbx - 2) + j, pl.ds(at, cells), :width] = rim[j]
+        first = e * (nbx - 3)
+        for j in range(3):
+            clamped_edges(fz, first + j, rows, width, 3 * c1)
+        for j in range(3):
+            forward_block(first + j, fz, hid, slope, wa)
     else:
+        blank_rims(fz)
         for s in range(count // 3):
             middle, before, after = pieces[3 * s : 3 * s + 3]
             at = pl.multiple_of(LAYERS + meta[s] * cells, LAYERS)
@@ -238,15 +275,12 @@
                 fz[nbx - 2 + j, pl.ds(at, cells), :width] = after[j]
             for j in range(nbx - 4):
                 fz[2 + j, pl.ds(at, cells), :width] = middle[j]
-    edges(fz, 0, nbx, rows, width, 3 * c1)
-    for j in range(nbx):
-        linear = combine(dot(taps(fz, j, 0, rows), wa[...]), width)
-        logistic = sigmoid(linear)
-        hid[j] = (linear * logistic).astype(BF)
-        slope[j] = logistic * (1.0 + linear * (1.0 - logistic))
+        edges(fz, 0, nbx, rows, width, 3 * c1)
+        for j in range(nbx):
+            forward_block(j, fz, hid, slope, wa)
     for j in range(nc + 2):
-        first, second = max(2 * j - 1, 0), min(2 * j, nbx - 1)
-        pooled = dot(paired_rows(hid[first], hid[second]), pool[...]) * 0.25
+        start, end = max(2 * j - 1, 0), min(2 * j, nbx - 1)
+        pooled = dot(paired_rows(hid[start], hid[end]), pool[...]) * 0.25
         cz[j, LAYERS : LAYERS + rows_c, :width] = keep_inside(meta, count // 3, pooled.astype(BF), 2)
     edges(cz, 1, nc + 1, rows_c, width, 3 * c1)
     for j in range(nc):
@@ -433,7 +467,7 @@
     gm_ref[...] = buf[c1:, 27 * c1 : 28 * c1].T
 
 
-def call(kernel, outs, *args, scratch=(), smem=0, near=(), far=()):
+def call(kernel, outs, *args, scratch=(), smem=0, near=(), far=(), aliases={}):
     args = list(args)
     specs = []
     for place in range(len(args)):
@@ -452,6 +486,7 @@
         in_specs=specs,
         out_specs=tuple(pl.BlockSpec(memory_space=pltpu.VMEM) for _ in outs),
         scratch_shapes=list(scratch),
+        input_output_aliases=aliases,
         compiler_params=pltpu.CompilerParams(vmem_limit_bytes=32 * 1024 * 1024),
     )(*args)
 
@@ -522,7 +557,7 @@
     block = (cells, width)
     f_own, c_own, first, second, *c_sent = call(
         functools.partial(pre_kernel, paired),
-        tuple(shape((n,) + block) for n in (nb, nb, 3, 3) + ((nb // 2 + 1,) if paired else ())),
+        tuple(pltpu.VMEM((n,) + block, BF) for n in (nb, nb, 3, 3) + ((nb // 2 + 1,) if paired else ())),
         features,
         cotangent,
         scratch=(
@@ -580,27 +615,31 @@
     skip = len(meta)
     count = len(f_pieces)
     matrices = (wa, wb, mp, pool)
+    fine = (
+        pltpu.VMEM((nbx, tall, 2 * width), BF),
+        pltpu.VMEM((nbx, rows, width), BF),
+        pltpu.VMEM((nbx, rows, width), F32),
+    )
+    pooled = (
+        pltpu.VMEM((nc + 2, tall_c, 2 * width), BF),
+        pltpu.VMEM((nc, rows_c, PB * c2), BF),
+        pltpu.VMEM((nc, rows_c, PB * c2), F32),
+        pltpu.VMEM((nc, rows_c, width), BF),
+    )
+    if paired:
+        started = call(chunk_kernel, fine, *f_pieces[:2], wa, near=range(3))
+        args = (*f_pieces[2:], *started, *matrices)
+        extra = {"near": range(len(args)), "aliases": {2: 0, 3: 1, 4: 2}}
+    else:
+        args = (*meta, *f_pieces, *matrices)
+        extra = {"near": range(skip + 1, len(args)), "smem": skip}
     fz, hid, slope, cz, gat, slope_b, proj = call(
-        functools.partial(forward_kernel, paired, count),
-        (
-            pltpu.VMEM((nbx, tall, 2 * width), BF),
-            pltpu.VMEM((nbx, rows, width), BF),
-            pltpu.VMEM((nbx, rows, width), F32),
-            pltpu.VMEM((nc + 2, tall_c, 2 * width), BF),
-            pltpu.VMEM((nc, rows_c, PB * c2), BF),
-            pltpu.VMEM((nc, rows_c, PB * c2), F32),
-            pltpu.VMEM((nc, rows_c, width), BF),
-        ),
-        *meta,
-        *f_pieces,
-        *matrices,
-        smem=skip,
-        near=range(skip + 1, skip + count + len(matrices)),
+        functools.partial(forward_kernel, paired, 2 if paired else count), fine + pooled, *args, **extra
     )
     inner = (fz, slope, cz, gat, slope_b, wbf, mt, pool, up)
     gz, terms = call(
         functools.partial(backward_kernel, paired, count),
-        (pltpu.VMEM((nbx, tall, 2 * width), BF), shape((devices, chunk, 128))),
+        (pltpu.VMEM((nbx, tall, 2 * width), BF), pltpu.VMEM((devices, chunk, 128), BF)),
         *meta,
         *c_pieces,
         *inner,
@@ -619,7 +658,7 @@
     blocks = 2 * (nbx - 4)
     results = call(
         functools.partial(finish_kernel, paired),
-        (shape((blocks, width, cells)),) * (2 if paired else 1),
+        (pltpu.VMEM((blocks, width, cells), BF),) * (2 if paired else 1),
         *meta,
         gz,
         hid,
@@ -634,12 +673,14 @@
         kept, sent = results
         received = lax.ppermute(sent, AXES, moves(lax.axis_size("phi"), 2, lambda p, s: (0, 1 - s)))
         terms, kept = lax.optimization_barrier((terms, kept))
-        output, grad_input = call(restore_kernel, (shape(features.shape), shape(features.shape)), kept, received)
+        output, grad_input = call(
+            restore_kernel, (shape(features.shape), shape(features.shape)), kept, received, near=(0, 1)
+        )
     else:
         output, grad_input = (
             jnp.transpose(part.reshape(n_rows, c1, cells), (1, 0, 2)) for part in (results[0][:nb], results[0][nb:])
         )
-    (sums,) = call(sum_kernel, (shape(terms.shape),), terms)
+    (sums,) = call(sum_kernel, (pltpu.VMEM(terms.shape, BF),), terms, near=(0,))
     sums = lax.all_to_all(sums, AXES, 0, 0, tiled=True)
     cell_count = n_rows * cells * devices
     grad_a, grad_b, grad_mix = call(
@@ -647,6 +688,7 @@
         (shape((27, c1, c1), F32), shape((27, c1, c2), F32), shape((c1, c2), F32)),
         sums,
         scratch=(pltpu.VMEM((c1 + c2, lanes), F32),),
+        near=(0,),
     )
     return output, grad_input, grad_a, jnp.swapaxes(grad_b, 1, 2), grad_mix
 

time: 47.4 us -> 46.8 us (0.987)
  waiting for transfers between devices: 17.1 us -> 16.5 us
    ppermute x4, waiting for transfers between devices: 1.14 us -> 0.54 us  [send(): return lax.ppermute(value, AXES, moves(n_phi, 2, rule))]
    pallas_call x8 -> x9, Pallas kernels: 12.4 us -> 12.7 us  [call(): pl.pallas_call(kernel, out_shape=outs, in_specs=specs, out_specs=tuple((p...]
  transfers between devices with their start and end apart: 7 -> 7, of which waited for: 5 -> 5; matrix products, arithmetic and copies ran while one was open for 0% -> 0% of each run, Pallas kernels for 13% -> 14%
where the time goes in v1:
time: 46.8 us; the launch traced here: 46.6 us
  starting transfers between devices  16.6 us (35%)
  waiting for transfers between devices  16.5 us (35%)
  Pallas kernels  12.7 us (27%)
  between operations  0.7 us (1%)
    pallas_call x9, Pallas kernels, call(): pl.pallas_call(kernel, out_shape=outs, in_specs=specs, out_specs=tuple((p...  12.7 us
    all_to_all x1, waiting for transfers between devices, shards(): terms = lax.all_to_all(terms, AXES, 0, 0, tiled=True)  8.89 us
    ppermute x4, starting transfers between devices, send(): return lax.ppermute(value, AXES, moves(n_phi, 2, rule))  7.65 us
    ppermute x1, waiting for transfers between devices, shards(): lax.ppermute(sent, AXES, moves(lax.axis_size('phi'), 2, lambda p, s: (0,...  5.46 us
    all_to_all x1, starting transfers between devices, shards(): terms = lax.all_to_all(terms, AXES, 0, 0, tiled=True)  4.67 us
    all_to_all x1, starting transfers between devices, shards(): sums = lax.all_to_all(sums, AXES, 0, 0, tiled=True)  2.58 us
    ppermute x1, starting transfers between devices, shards(): lax.ppermute(sent, AXES, moves(lax.axis_size('phi'), 2, lambda p, s: (0,...  1.72 us
    all_to_all x1, waiting for transfers between devices, shards(): sums = lax.all_to_all(sums, AXES, 0, 0, tiled=True)  1.66 us
  transfers between devices with their start and end apart: 7, of which 5 were waited for; matrix products, arithmetic and copies ran while one was open for 0% of the time, Pallas kernels for 14%

profile of v1, /device:TPU:0, one launch (start us, length us, event | category | flops | bytes accessed | tf_op | source)
XLA Modules:
  0.0 46.6 jit_solution(634074392150960048)
XLA Ops:
  0.6 1.2 %shard_map.92 = (bf16[4,128,128]{2,1,0:T(8,128)(2,1)S(1)}, bf16[4,128,128]{2,1,0:T(8,128)(2,1)S(1)}, bf16[3,128,128]{2,1,0:T(8,128)(2,1)S(1)}, bf16[3,128,128]{2,1,0:T(8,128)(2,1)S(1)}, bf16[3,128,128]{2,1,0:T(8,128)(2,1)S(1)}) custom-call(bf16[32,16,128]{2,1,0:T(8,128)(2,1)} %f_hbm.1, bf16[32,16,128]{2,1,0:T(8,128)(2,1)} %c_hbm.1), custom_call_target="tpu_custom_call" | custom-call | tf_op jit(solution)/shard_map/pallas_call | solution.py:483
  1.9 3.1 %collective-permute-start.3 = (bf16[4,128,128]{2,1,0:T(8,128)(2,1)S(1)}, bf16[4,128,128]{2,1,0:T(8,128)(2,1)S(1)}, u32[]{:S(2)}, u32[]{:S(2)}) collective-permute-start(bf16[4,128,128]{2,1,0:T(8,128)(2,1)S(1)} %get-tuple-element.43.own), channel_id=1, source_target_pairs={{0,1},{1,0},{2,3},{3,2},{4,5},{5,4},{6,7},{7,6},{8,9},{9,8},{10,11... | collective-permute-start | bytes 393224 | tf_op jit(solution)/shard_map/ppermute | solution.py:515
  4.9 0.0 collective-permute-start.1
  4.9 4.6 %collective-permute-start.2 = (bf16[3,128,128]{2,1,0:T(8,128)(2,1)S(1)}, bf16[3,128,128]{2,1,0:T(8,128)(2,1)S(1)}, u32[]{:S(2)}, u32[]{:S(2)}) collective-permute-start(bf16[3,128,128]{2,1,0:T(8,128)(2,1)S(1)} %get-tuple-element.42), channel_id=1, source_target_pairs={{0,31},{1,2},{2,1},{3,4},{4,3},{5,6},{6,5},{7,8},{8,7},{9,10},{10,... | collective-permute-start | bytes 294920 | tf_op jit(solution)/shard_map/ppermute | solution.py:515
  9.5 0.0 collective-permute-start
  9.5 2.0 %shard_map.93 = (bf16[768,384]{1,0:T(8,128)(2,1)S(1)}, bf16[768,384]{1,0:T(8,128)(2,1)S(1)}, bf16[768,768]{1,0:T(8,128)(2,1)S(1)}, bf16[1152,384]{1,0:T(8,128)(2...) custom-call(bf16[27,32,32]{2,1,0:T(8,128)(2,1)} %ka_hbm.1, ...), custom_call_target="tpu_custom_call" | custom-call | tf_op jit(solution)/shard_map/pallas_call | solution.py:483
  11.6 0.0 collective-permute-done.3.partner
  11.6 0.9 %shard_map.94 = (bf16[6,320,256]{2,1,0:T(8,128)(2,1)S(1)}, bf16[6,256,128]{2,1,0:T(8,128)(2,1)S(1)}, f32[6,256,128]{2,1,0:T(8,128)S(1)}) custom-call(bf16[4,128,128]{2,1,0:T(8,128)(2,1)S(1)} %get-tuple-element.43.own, bf16[4,128,128]{2,1,0:T(8,128)(2,1)S(1)} %collective-permute-done.3.partner, bf16[768,384]{1,0:T(8,128)(2,1)S(1)} %get-tuple-element.44.wa.refs_5_), custom_call_target="tpu_custom_call" | custom-call | tf_op jit(solution)/shard_map/pallas_call | solution.py:483
  12.4 0.0 collective-permute-done.1.refs_0_.refs_2_
  12.5 0.2 collective-permute-done.2.refs_1_.refs_3_
  12.7 1.9 %shard_map.95 = (bf16[6,320,256]{2,1,0:T(8,128)(2,1)S(1)}, bf16[6,256,128]{2,1,0:T(8,128)(2,1)S(1)}, f32[6,256,128]{2,1,0:T(8,128)S(1)}, bf16[4,192,256]{2,1,0:T...) custom-call(bf16[3,128,128]{2,1,0:T(8,128)(2,1)S(1)} %collective-per, ...), custom_call_target="tpu_custom_call", output_to_operand_aliasing={{0}: (2, {}), {1}: (3, {}), {2}: (4, {})} | custom-call | tf_op jit(solution)/shard_map/pallas_call | solution.py:483
  14.6 0.3 collective-permute-done.refs_1_
  14.9 3.1 %shard_map.96 = (bf16[6,320,256]{2,1,0:T(8,128)(2,1)S(1)}, bf16[32,24,128]{2,1,0:T(8,128)(2,1)}) custom-call(bf16[4,128,128]{2,1,0:T(8,128)(2,1)S(1)} %get-tuple-element.39.refs_0_, bf16[3,128,128]{2,1,0:T(8,128)(2,1)S(1)} %collective-permute-done.refs_1_, bf16[3,128,128]{2,1,0:T(8,128)(2,1)S(1)} %collective-permute-done.1.refs_0_.refs_2_, ...), custom_call_target="tpu_custom_call" | custom-call | tf_op jit(solution)/shard_map/pallas_call | solution.py:483
  18.0 4.7 %all-to-all-start = ((bf16[32,24,128]{2,1,0:T(8,128)(2,1)}), bf16[32,24,128]{2,1,0:T(8,128)(2,1)S(1)}, u32[]{:S(2)}, u32[]{:S(2)}) async-start(bf16[32,24,128]{2,1,0:T(8,128)(2,1)} %get-tuple-element.59), calls=%async_computation | async-start | bytes 393216 | tf_op jit(solution)/shard_map/all_to_all | solution.py:657
  22.6 0.7 %shard_map.97 = (bf16[4,128,128]{2,1,0:T(8,128)(2,1)S(1)}, bf16[4,128,128]{2,1,0:T(8,128)(2,1)S(1)}) custom-call(bf16[6,320,256]{2,1,0:T(8,128)(2,1)S(1)} %get-tuple-element.60.refs_0_, bf16[6,256,128]{2,1,0:T(8,128)(2,1)S(1)} %get-tuple-element.61.refs_1_, bf16[2,128,128]{2,1,0:T(8,128)(2,1)S(1)} %get-tuple-element.62.refs_2_, ...), custom_call_target="tpu_custom_call" | custom-call | tf_op jit(solution)/shard_map/pallas_call | solution.py:483
  23.4 8.9 %all-to-all-done.x_ref = bf16[32,24,128]{2,1,0:T(8,128)(2,1)S(1)} async-done(((bf16[32,24,128]{2,1,0:T(8,128)(2,1)}), bf16[32,24,128]{2,1,0:T(8,128)(2,1)S(1)}, u32[]{:S(2)}, u32[]{:S(2)}) %all-to-all-start) | async-done | bytes 196640 | tf_op jit(solution)/shard_map/all_to_all | solution.py:657
  32.3 0.7 %shard_map.99 = bf16[32,24,128]{2,1,0:T(8,128)(2,1)} custom-call(bf16[32,24,128]{2,1,0:T(8,128)(2,1)S(1)} %all-to-all-done.x_ref), custom_call_target="tpu_custom_call" | custom-call | tf_op jit(solution)/shard_map/pallas_call | solution.py:483
  33.0 2.6 %all-to-all-start.1 = ((bf16[32,24,128]{2,1,0:T(8,128)(2,1)}), bf16[32,24,128]{2,1,0:T(8,128)(2,1)S(1)}, u32[]{:S(2)}, u32[]{:S(2)}) async-start(bf16[32,24,128]{2,1,0:T(8,128)(2,1)} %shard_map.99), calls=%async_computation.1 | async-start | bytes 393216 | tf_op jit(solution)/shard_map/all_to_all | solution.py:684
  35.6 1.7 %collective-permute-start.4 = (bf16[4,128,128]{2,1,0:T(8,128)(2,1)S(1)}, bf16[4,128,128]{2,1,0:T(8,128)(2,1)S(1)}, u32[]{:S(2)}, u32[]{:S(2)}) collective-permute-start(bf16[4,128,128]{2,1,0:T(8,128)(2,1)S(1)} %get-tuple-element.66), channel_id=1, source_target_pairs={{0,1},{1,0},{2,3},{3,2},{4,5},{5,4},{6,7},{7,6},{8,9},{9,8},{10,11... | collective-permute-start | bytes 393224 | tf_op jit(solution)/shard_map/ppermute | solution.py:674
  37.3 5.5 %collective-permute-done.4.received = bf16[4,128,128]{2,1,0:T(8,128)(2,1)S(1)} collective-permute-done((bf16[4,128,128]{2,1,0:T(8,128)(2,1)S(1)}, bf16[4,128,128]{2,1,0:T(8,128)(2,1)S(1)}, u32[]{:S(2)}, u32[]{:S(2)}) %collective-permute-start.4) | collective-permute-done | bytes 131104 | tf_op jit(solution)/shard_map/ppermute | solution.py:674
  42.8 0.8 %shard_map.98 = (bf16[32,16,128]{2,1,0:T(8,128)(2,1)}, bf16[32,16,128]{2,1,0:T(8,128)(2,1)}) custom-call(bf16[4,128,128]{2,1,0:T(8,128)(2,1)S(1)} %get-tuple-element.65.kept, bf16[4,128,128]{2,1,0:T(8,128)(2,1)S(1)} %collective-permute-done.4.received), custom_call_target="tpu_custom_call" | custom-call | tf_op jit(solution)/shard_map/pallas_call | solution.py:483
  43.6 1.7 %all-to-all-done.1.x_ref = bf16[32,24,128]{2,1,0:T(8,128)(2,1)S(1)} async-done(((bf16[32,24,128]{2,1,0:T(8,128)(2,1)}), bf16[32,24,128]{2,1,0:T(8,128)(2,1)S(1)}, u32[]{:S(2)}, u32[]{:S(2)}) %all-to-all-start.1) | async-done | bytes 196640 | tf_op jit(solution)/shard_map/all_to_all | solution.py:684
  45.2 1.4 %shard_map.100 = (f32[27,32,32]{2,1,0:T(8,128)}, f32[27,32,64]{2,1,0:T(8,128)}, f32[32,64]{1,0:T(8,128)}) custom-call(bf16[32,24,128]{2,1,0:T(8,128)(2,1)S(1)} %all-to-all-done.1.x_ref), custom_call_target="tpu_custom_call" | custom-call | tf_op jit(solution)/shard_map/pallas_call | solution.py:483
Async XLA Ops:
  1.9 9.7 %collective-permute-start.3 = (bf16[4,128,128]{2,1,0:T(8,128)(2,1)S(1)}, bf16[4,128,128]{2,1,0:T(8,128)(2,1)S(1)}, u32[]{:S(2)}, u32[]{:S(2)}) collective-permute-start(bf16[4,128,128]{2,1,0:T(8,128)(2,1)S(1)} %get-tuple-element.43.own), channel_id=1, source_target_pairs={{0,1},{1,0},{2,3},{3,2},{4,5},{5,4},{6,7},{7,6},{8,9},{9,8},{10,11... | collective-permute-start | bytes 393224 | tf_op jit(solution)/shard_map/ppermute | solution.py:515
  4.9 7.5 %collective-permute-start.1 = (bf16[3,128,128]{2,1,0:T(8,128)(2,1)S(1)}, bf16[3,128,128]{2,1,0:T(8,128)(2,1)S(1)}, u32[]{:S(2)}, u32[]{:S(2)}) collective-permute-start(bf16[3,128,128]{2,1,0:T(8,128)(2,1)S(1)} %get-tuple-element.41), channel_id=1, source_target_pairs={{0,2},{1,31},{2,4},{3,1},{4,6},{5,3},{6,8},{7,5},{8,10},{9,7},{10,... | collective-permute-start | bytes 294920 | tf_op jit(solution)/shard_map/ppermute | solution.py:515
  4.9 7.7 %collective-permute-start.2 = (bf16[3,128,128]{2,1,0:T(8,128)(2,1)S(1)}, bf16[3,128,128]{2,1,0:T(8,128)(2,1)S(1)}, u32[]{:S(2)}, u32[]{:S(2)}) collective-permute-start(bf16[3,128,128]{2,1,0:T(8,128)(2,1)S(1)} %get-tuple-element.42), channel_id=1, source_target_pairs={{0,31},{1,2},{2,1},{3,4},{4,3},{5,6},{6,5},{7,8},{8,7},{9,10},{10,... | collective-permute-start | bytes 294920 | tf_op jit(solution)/shard_map/ppermute | solution.py:515
  9.5 5.4 %collective-permute-start = (bf16[3,128,128]{2,1,0:T(8,128)(2,1)S(1)}, bf16[3,128,128]{2,1,0:T(8,128)(2,1)S(1)}, u32[]{:S(2)}, u32[]{:S(2)}) collective-permute-start(bf16[3,128,128]{2,1,0:T(8,128)(2,1)S(1)} %get-tuple-element.40), channel_id=1, source_target_pairs={{0,1},{1,0},{2,3},{3,2},{4,5},{5,4},{6,7},{7,6},{8,9},{9,8},{10,11... | collective-permute-start | bytes 294920 | tf_op jit(solution)/shard_map/ppermute | solution.py:515
  18.0 14.3 %all-to-all-start = ((bf16[32,24,128]{2,1,0:T(8,128)(2,1)}), bf16[32,24,128]{2,1,0:T(8,128)(2,1)S(1)}, u32[]{:S(2)}, u32[]{:S(2)}) async-start(bf16[32,24,128]{2,1,0:T(8,128)(2,1)} %get-tuple-element.59), calls=%async_computation | async-start | bytes 393216 | tf_op jit(solution)/shard_map/all_to_all | solution.py:657
  33.0 12.2 %all-to-all-start.1 = ((bf16[32,24,128]{2,1,0:T(8,128)(2,1)}), bf16[32,24,128]{2,1,0:T(8,128)(2,1)S(1)}, u32[]{:S(2)}, u32[]{:S(2)}) async-start(bf16[32,24,128]{2,1,0:T(8,128)(2,1)} %shard_map.99), calls=%async_computation.1 | async-start | bytes 393216 | tf_op jit(solution)/shard_map/all_to_all | solution.py:684
  35.6 7.2 %collective-permute-start.4 = (bf16[4,128,128]{2,1,0:T(8,128)(2,1)S(1)}, bf16[4,128,128]{2,1,0:T(8,128)(2,1)S(1)}, u32[]{:S(2)}, u32[]{:S(2)}) collective-permute-start(bf16[4,128,128]{2,1,0:T(8,128)(2,1)S(1)} %get-tuple-element.66), channel_id=1, source_target_pairs={{0,1},{1,0},{2,3},{3,2},{4,5},{5,4},{6,7},{7,6},{8,9},{9,8},{10,11... | collective-permute-start | bytes 393224 | tf_op jit(solution)/shard_map/ppermute | solution.py:674

commit v2 on v1

--- a/solution.py
+++ b/solution.py
@@ -83,7 +83,7 @@
     tb[...] = dot(flat(kbt[...]), many)
     tbf[...] = dot(flat(turned(kbt)), few)
 
-    def toeplitz(out, source, order, rows_per, cols_per, row_blocks):
+    def toeplitz(out, source, order, rows_per, cols_per, row_blocks, turn=0):
         height = len(row_blocks) * rows_per
         across = PB * cols_per
         place = iota((rows_per, across), 1) // cols_per
@@ -92,14 +92,15 @@
                 for at, q in enumerate(row_blocks):
                     value = jnp.zeros((rows_per, across), F32)
                     for a in range(3):
-                        if 0 <= q + 1 - a < PB:
+                        p = q + 1 - a
+                        if 0 <= p < PB:
                             t = order(9 * a + 3 * b + c) * rows_per
-                            value = jnp.where(place == q + 1 - a, source[t : t + rows_per], value)
+                            value = jnp.where(place == (p + turn) % PB, source[t : t + rows_per], value)
                     first = b * height + at * rows_per
                     out[first : first + rows_per, c * across : (c + 1) * across] = value.astype(BF)
 
     ring = (0, 1, 2, 3, 4, 100, 100, -1)
-    toeplitz(wa, ta, lambda t: t, c1, c1, ring)
+    toeplitz(wa, ta, lambda t: t, c1, c1, (2, 3, 0, 1, 100, -1, 4, 100), PB // 2)
     toeplitz(wb, tb, lambda t: t, c1, c2, ring)
     toeplitz(wbf, tbf, lambda t: 26 - t, c2, c1, (0, 1, 2, 3, 4, -1))
     toeplitz(waf, taf, lambda t: 26 - t, c1, c1, ring)
@@ -202,37 +203,43 @@
     return jnp.where(inside, value, jnp.zeros_like(value))
 
 
-def clamped_edges(ref, j, inner, width, split):
-    lane = iota((inner, width), 1)
-    at = slice(LAYERS, LAYERS + inner)
-    nxt = ref[jnp.minimum(j + 1, ref.shape[0] - 1), at, :width]
-    prv = ref[jnp.maximum(j - 1, 0), at, :width]
-    ref[j, at, width:] = jnp.where(lane < split, nxt, prv)
-
-
-def forward_block(j, fz, hid, slope, wa):
+def forward_block(place, j, fz, half_way, hid, slope, wa):
     rows, width = hid.shape[1:]
-    linear = combine(dot(taps(fz, j, 0, rows), wa[...]), width)
+    half = width // 2
+    at = slice(LAYERS, LAYERS + rows)
+    left = iota((rows, width), 1) < half
+    low, high = fz[j, at, :width], fz[j + 1, at, :width]
+    half_way[place, at, :width] = jnp.where(left, high, low)
+    half_way[place, at, width:] = jnp.where(left, low, high)
+    linear = combine(dot(taps(half_way, place, 0, rows), wa[...]), width)
     logistic = sigmoid(linear)
-    hid[j] = (linear * logistic).astype(BF)
-    slope[j] = logistic * (1.0 + linear * (1.0 - logistic))
-
-
-def chunk_kernel(own, partner, wa, fz, hid, slope):
+    hidden = (linear * logistic).astype(BF)
+    steep = logistic * (1.0 + linear * (1.0 - logistic))
+    for ref, value in ((hid, hidden), (slope, steep)):
+        ref[j + 1, :, :half] = value[:, :half]
+        ref[j, :, half:] = value[:, half:]
+
+
+def blank_ends(hid):
+    rows, width = hid.shape[1:]
+    none = jnp.zeros((rows, width // 2), BF)
+    hid[0, :, : width // 2] = none
+    hid[hid.shape[0] - 1, :, width // 2 :] = none
+
+
+def chunk_kernel(own, partner, wa, fz, hid, slope, half_way):
     nbx = fz.shape[0]
     nb, cells, width = own.shape
-    rows = hid.shape[1]
     e = lax.axis_index("eta")
     blank_rims(fz)
+    blank_rims(half_way)
+    blank_ends(hid)
     for chunk, shard in ((own, e), (partner, 1 - e)):
         at = pl.multiple_of(LAYERS + shard * cells, LAYERS)
         for j in range(nb // 2 + 2):
             fz[j + 2 * (1 - e), pl.ds(at, cells), :width] = chunk[j + e * (nb // 2 - 2)]
-    first = 3 * (1 - e)
     for j in range(nbx - 3):
-        clamped_edges(fz, first + j, rows, width, 3 * width // PB)
-    for j in range(nbx - 3):
-        forward_block(first + j, fz, hid, slope, wa)
+        forward_block(j, 2 * (1 - e) + j, fz, half_way, hid, slope, wa)
 
 
 def forward_kernel(paired, count, *refs):
@@ -243,7 +250,7 @@
     if paired:
         refs = refs[3:]
     wa, wb, mp, pool = refs[:4]
-    fz, hid, slope, cz, gat, slope_b, proj = refs[4:]
+    fz, hid, slope, cz, gat, slope_b, proj, half_way = refs[4:]
     nbx = fz.shape[0]
     nc = gat.shape[0]
     rows = hid.shape[1]
@@ -252,6 +259,7 @@
     c1 = width // PB
     wide = gat.shape[2]
     blank_rims(cz)
+    blank_rims(half_way)
     cells = pieces[0].shape[1]
     if paired:
         near, far = pieces
@@ -260,13 +268,11 @@
             at = pl.multiple_of(LAYERS + shard * cells, LAYERS)
             for j in range(2):
                 fz[e * (nbx - 2) + j, pl.ds(at, cells), :width] = rim[j]
-        first = e * (nbx - 3)
-        for j in range(3):
-            clamped_edges(fz, first + j, rows, width, 3 * c1)
-        for j in range(3):
-            forward_block(first + j, fz, hid, slope, wa)
+        for j in range(2):
+            forward_block(j, e * (nbx - 3) + j, fz, half_way, hid, slope, wa)
     else:
         blank_rims(fz)
+        blank_ends(hid)
         for s in range(count // 3):
             middle, before, after = pieces[3 * s : 3 * s + 3]
             at = pl.multiple_of(LAYERS + meta[s] * cells, LAYERS)
@@ -275,9 +281,9 @@
                 fz[nbx - 2 + j, pl.ds(at, cells), :width] = after[j]
             for j in range(nbx - 4):
                 fz[2 + j, pl.ds(at, cells), :width] = middle[j]
-        edges(fz, 0, nbx, rows, width, 3 * c1)
-        for j in range(nbx):
-            forward_block(j, fz, hid, slope, wa)
+        for j in range(nbx - 1):
+            forward_block(j, j, fz, half_way, hid, slope, wa)
+    edges(fz, 2, nbx - 2, rows, width, 3 * c1)
     for j in range(nc + 2):
         start, end = max(2 * j - 1, 0), min(2 * j, nbx - 1)
         pooled = dot(paired_rows(hid[start], hid[end]), pool[...]) * 0.25
@@ -626,15 +632,20 @@
         pltpu.VMEM((nc, rows_c, PB * c2), F32),
         pltpu.VMEM((nc, rows_c, width), BF),
     )
+    between = lambda n: (pltpu.VMEM((n, tall, 2 * width), BF),)
     if paired:
-        started = call(chunk_kernel, fine, *f_pieces[:2], wa, near=range(3))
+        started = call(chunk_kernel, fine, *f_pieces[:2], wa, scratch=between(nbx - 3), near=range(3))
         args = (*f_pieces[2:], *started, *matrices)
         extra = {"near": range(len(args)), "aliases": {2: 0, 3: 1, 4: 2}}
     else:
         args = (*meta, *f_pieces, *matrices)
         extra = {"near": range(skip + 1, len(args)), "smem": skip}
     fz, hid, slope, cz, gat, slope_b, proj = call(
-        functools.partial(forward_kernel, paired, 2 if paired else count), fine + pooled, *args, **extra
+        functools.partial(forward_kernel, paired, 2 if paired else count),
+        fine + pooled,
+        *args,
+        scratch=between(2 if paired else nbx - 1),
+        **extra,
     )
     inner = (fz, slope, cz, gat, slope_b, wbf, mt, pool, up)
     gz, terms = call(

time: 46.8 us -> 46.7 us (level)
  transfers between devices with their start and end apart: 7 -> 7, of which waited for: 5 -> 5; matrix products, arithmetic and copies ran while one was open for 0% -> 0% of each run, Pallas kernels for 14% -> 13%
where the time goes in v2:
time: 46.7 us; the launch traced here: 46.4 us
  waiting for transfers between devices  16.7 us (36%)
  starting transfers between devices  16.4 us (35%)
  Pallas kernels  12.5 us (27%)
  between operations  0.7 us (1%)
    pallas_call x9, Pallas kernels, call(): pl.pallas_call(kernel, out_shape=outs, in_specs=specs, out_specs=tuple((p...  12.5 us
    all_to_all x1, waiting for transfers between devices, shards(): terms = lax.all_to_all(terms, AXES, 0, 0, tiled=True)  8.89 us
    ppermute x4, starting transfers between devices, send(): return lax.ppermute(value, AXES, moves(n_phi, 2, rule))  7.65 us
    ppermute x1, waiting for transfers between devices, shards(): lax.ppermute(sent, AXES, moves(lax.axis_size('phi'), 2, lambda p, s: (0,...  5.46 us
    all_to_all x1, starting transfers between devices, shards(): terms = lax.all_to_all(terms, AXES, 0, 0, tiled=True)  4.5 us
    all_to_all x1, starting transfers between devices, shards(): sums = lax.all_to_all(sums, AXES, 0, 0, tiled=True)  2.58 us
    ppermute x1, starting transfers between devices, shards(): lax.ppermute(sent, AXES, moves(lax.axis_size('phi'), 2, lambda p, s: (0,...  1.72 us
    all_to_all x1, waiting for transfers between devices, shards(): sums = lax.all_to_all(sums, AXES, 0, 0, tiled=True)  1.66 us
  transfers between devices with their start and end apart: 7, of which 5 were waited for; matrix products, arithmetic and copies ran while one was open for 0% of the time, Pallas kernels for 13%

profile of v2, /device:TPU:0, one launch (start us, length us, event | category | flops | bytes accessed | tf_op | source)
XLA Modules:
  0.0 46.4 jit_solution(6468928243845919968)
XLA Ops:
  0.6 1.2 %shard_map.92 = (bf16[4,128,128]{2,1,0:T(8,128)(2,1)S(1)}, bf16[4,128,128]{2,1,0:T(8,128)(2,1)S(1)}, bf16[3,128,128]{2,1,0:T(8,128)(2,1)S(1)}, bf16[3,128,128]{2,1,0:T(8,128)(2,1)S(1)}, bf16[3,128,128]{2,1,0:T(8,128)(2,1)S(1)}) custom-call(bf16[32,16,128]{2,1,0:T(8,128)(2,1)} %f_hbm.1, bf16[32,16,128]{2,1,0:T(8,128)(2,1)} %c_hbm.1), custom_call_target="tpu_custom_call" | custom-call | tf_op jit(solution)/shard_map/pallas_call | solution.py:489
  1.9 3.1 %collective-permute-start.3 = (bf16[4,128,128]{2,1,0:T(8,128)(2,1)S(1)}, bf16[4,128,128]{2,1,0:T(8,128)(2,1)S(1)}, u32[]{:S(2)}, u32[]{:S(2)}) collective-permute-start(bf16[4,128,128]{2,1,0:T(8,128)(2,1)S(1)} %get-tuple-element.43.own), channel_id=1, source_target_pairs={{0,1},{1,0},{2,3},{3,2},{4,5},{5,4},{6,7},{7,6},{8,9},{9,8},{10,11... | collective-permute-start | bytes 393224 | tf_op jit(solution)/shard_map/ppermute | solution.py:521
  4.9 0.0 collective-permute-start.1
  4.9 4.6 %collective-permute-start.2 = (bf16[3,128,128]{2,1,0:T(8,128)(2,1)S(1)}, bf16[3,128,128]{2,1,0:T(8,128)(2,1)S(1)}, u32[]{:S(2)}, u32[]{:S(2)}) collective-permute-start(bf16[3,128,128]{2,1,0:T(8,128)(2,1)S(1)} %get-tuple-element.42), channel_id=1, source_target_pairs={{0,31},{1,2},{2,1},{3,4},{4,3},{5,6},{6,5},{7,8},{8,7},{9,10},{10,... | collective-permute-start | bytes 294920 | tf_op jit(solution)/shard_map/ppermute | solution.py:521
  9.5 0.0 collective-permute-start
  9.5 2.0 %shard_map.93 = (bf16[768,384]{1,0:T(8,128)(2,1)S(1)}, bf16[768,384]{1,0:T(8,128)(2,1)S(1)}, bf16[768,768]{1,0:T(8,128)(2,1)S(1)}, bf16[1152,384]{1,0:T(8,128)(2...) custom-call(bf16[27,32,32]{2,1,0:T(8,128)(2,1)} %ka_hbm.1, ...), custom_call_target="tpu_custom_call" | custom-call | tf_op jit(solution)/shard_map/pallas_call | solution.py:489
  11.6 0.0 collective-permute-done.3.partner
  11.6 0.9 %shard_map.94 = (bf16[6,320,256]{2,1,0:T(8,128)(2,1)S(1)}, bf16[6,256,128]{2,1,0:T(8,128)(2,1)S(1)}, f32[6,256,128]{2,1,0:T(8,128)S(1)}) custom-call(bf16[4,128,128]{2,1,0:T(8,128)(2,1)S(1)} %get-tuple-element.43.own, bf16[4,128,128]{2,1,0:T(8,128)(2,1)S(1)} %collective-permute-done.3.partner, bf16[768,384]{1,0:T(8,128)(2,1)S(1)} %get-tuple-element.44.wa.refs_5_), custom_call_target="tpu_custom_call" | custom-call | tf_op jit(solution)/shard_map/pallas_call | solution.py:489
  12.4 0.0 collective-permute-done.1.refs_0_.refs_2_
  12.4 0.2 collective-permute-done.2.refs_1_.refs_3_
  12.7 1.7 %shard_map.95 = (bf16[6,320,256]{2,1,0:T(8,128)(2,1)S(1)}, bf16[6,256,128]{2,1,0:T(8,128)(2,1)S(1)}, f32[6,256,128]{2,1,0:T(8,128)S(1)}, bf16[4,192,256]{2,1,0:T...) custom-call(bf16[3,128,128]{2,1,0:T(8,128)(2,1)S(1)} %collective-per, ...), custom_call_target="tpu_custom_call", output_to_operand_aliasing={{0}: (2, {}), {1}: (3, {}), {2}: (4, {})} | custom-call | tf_op jit(solution)/shard_map/pallas_call | solution.py:489
  14.4 0.5 %collective-permute-done.refs_1_ = bf16[3,128,128]{2,1,0:T(8,128)(2,1)S(1)} collective-permute-done((bf16[3,128,128]{2,1,0:T(8,128)(2,1)S(1)}, bf16[3,128,128]{2,1,0:T(8,128)(2,1)S(1)}, u32[]{:S(2)}, u32[]{:S(2)}) %collective-permute-start) | collective-permute-done | bytes 98336 | tf_op jit(solution)/shard_map/ppermute | solution.py:521
  14.9 3.1 %shard_map.96 = (bf16[6,320,256]{2,1,0:T(8,128)(2,1)S(1)}, bf16[32,24,128]{2,1,0:T(8,128)(2,1)}) custom-call(bf16[4,128,128]{2,1,0:T(8,128)(2,1)S(1)} %get-tuple-element.39.refs_0_, bf16[3,128,128]{2,1,0:T(8,128)(2,1)S(1)} %collective-permute-done.refs_1_, bf16[3,128,128]{2,1,0:T(8,128)(2,1)S(1)} %collective-permute-done.1.refs_0_.refs_2_, ...), custom_call_target="tpu_custom_call" | custom-call | tf_op jit(solution)/shard_map/pallas_call | solution.py:489
  18.0 4.5 %all-to-all-start = ((bf16[32,24,128]{2,1,0:T(8,128)(2,1)}), bf16[32,24,128]{2,1,0:T(8,128)(2,1)S(1)}, u32[]{:S(2)}, u32[]{:S(2)}) async-start(bf16[32,24,128]{2,1,0:T(8,128)(2,1)} %get-tuple-element.59), calls=%async_computation | async-start | bytes 393216 | tf_op jit(solution)/shard_map/all_to_all | solution.py:668
  22.5 0.7 %shard_map.97 = (bf16[4,128,128]{2,1,0:T(8,128)(2,1)S(1)}, bf16[4,128,128]{2,1,0:T(8,128)(2,1)S(1)}) custom-call(bf16[6,320,256]{2,1,0:T(8,128)(2,1)S(1)} %get-tuple-element.60.refs_0_, bf16[6,256,128]{2,1,0:T(8,128)(2,1)S(1)} %get-tuple-element.61.refs_1_, bf16[2,128,128]{2,1,0:T(8,128)(2,1)S(1)} %get-tuple-element.62.refs_2_, ...), custom_call_target="tpu_custom_call" | custom-call | tf_op jit(solution)/shard_map/pallas_call | solution.py:489
  23.2 8.9 %all-to-all-done.x_ref = bf16[32,24,128]{2,1,0:T(8,128)(2,1)S(1)} async-done(((bf16[32,24,128]{2,1,0:T(8,128)(2,1)}), bf16[32,24,128]{2,1,0:T(8,128)(2,1)S(1)}, u32[]{:S(2)}, u32[]{:S(2)}) %all-to-all-start) | async-done | bytes 196640 | tf_op jit(solution)/shard_map/all_to_all | solution.py:668
  32.1 0.7 %shard_map.99 = bf16[32,24,128]{2,1,0:T(8,128)(2,1)} custom-call(bf16[32,24,128]{2,1,0:T(8,128)(2,1)S(1)} %all-to-all-done.x_ref), custom_call_target="tpu_custom_call" | custom-call | tf_op jit(solution)/shard_map/pallas_call | solution.py:489
  32.8 2.6 %all-to-all-start.1 = ((bf16[32,24,128]{2,1,0:T(8,128)(2,1)}), bf16[32,24,128]{2,1,0:T(8,128)(2,1)S(1)}, u32[]{:S(2)}, u32[]{:S(2)}) async-start(bf16[32,24,128]{2,1,0:T(8,128)(2,1)} %shard_map.99), calls=%async_computation.1 | async-start | bytes 393216 | tf_op jit(solution)/shard_map/all_to_all | solution.py:695
  35.4 1.7 %collective-permute-start.4 = (bf16[4,128,128]{2,1,0:T(8,128)(2,1)S(1)}, bf16[4,128,128]{2,1,0:T(8,128)(2,1)S(1)}, u32[]{:S(2)}, u32[]{:S(2)}) collective-permute-start(bf16[4,128,128]{2,1,0:T(8,128)(2,1)S(1)} %get-tuple-element.66), channel_id=1, source_target_pairs={{0,1},{1,0},{2,3},{3,2},{4,5},{5,4},{6,7},{7,6},{8,9},{9,8},{10,11... | collective-permute-start | bytes 393224 | tf_op jit(solution)/shard_map/ppermute | solution.py:685
  37.1 5.5 %collective-permute-done.4.received = bf16[4,128,128]{2,1,0:T(8,128)(2,1)S(1)} collective-permute-done((bf16[4,128,128]{2,1,0:T(8,128)(2,1)S(1)}, bf16[4,128,128]{2,1,0:T(8,128)(2,1)S(1)}, u32[]{:S(2)}, u32[]{:S(2)}) %collective-permute-start.4) | collective-permute-done | bytes 131104 | tf_op jit(solution)/shard_map/ppermute | solution.py:685
  42.6 0.8 %shard_map.98 = (bf16[32,16,128]{2,1,0:T(8,128)(2,1)}, bf16[32,16,128]{2,1,0:T(8,128)(2,1)}) custom-call(bf16[4,128,128]{2,1,0:T(8,128)(2,1)S(1)} %get-tuple-element.65.kept, bf16[4,128,128]{2,1,0:T(8,128)(2,1)S(1)} %collective-permute-done.4.received), custom_call_target="tpu_custom_call" | custom-call | tf_op jit(solution)/shard_map/pallas_call | solution.py:489
  43.4 1.7 %all-to-all-done.1.x_ref = bf16[32,24,128]{2,1,0:T(8,128)(2,1)S(1)} async-done(((bf16[32,24,128]{2,1,0:T(8,128)(2,1)}), bf16[32,24,128]{2,1,0:T(8,128)(2,1)S(1)}, u32[]{:S(2)}, u32[]{:S(2)}) %all-to-all-start.1) | async-done | bytes 196640 | tf_op jit(solution)/shard_map/all_to_all | solution.py:695
  45.1 1.4 %shard_map.100 = (f32[27,32,32]{2,1,0:T(8,128)}, f32[27,32,64]{2,1,0:T(8,128)}, f32[32,64]{1,0:T(8,128)}) custom-call(bf16[32,24,128]{2,1,0:T(8,128)(2,1)S(1)} %all-to-all-done.1.x_ref), custom_call_target="tpu_custom_call" | custom-call | tf_op jit(solution)/shard_map/pallas_call | solution.py:489
Async XLA Ops:
  1.9 9.7 %collective-permute-start.3 = (bf16[4,128,128]{2,1,0:T(8,128)(2,1)S(1)}, bf16[4,128,128]{2,1,0:T(8,128)(2,1)S(1)}, u32[]{:S(2)}, u32[]{:S(2)}) collective-permute-start(bf16[4,128,128]{2,1,0:T(8,128)(2,1)S(1)} %get-tuple-element.43.own), channel_id=1, source_target_pairs={{0,1},{1,0},{2,3},{3,2},{4,5},{5,4},{6,7},{7,6},{8,9},{9,8},{10,11... | collective-permute-start | bytes 393224 | tf_op jit(solution)/shard_map/ppermute | solution.py:521
  4.9 7.5 %collective-permute-start.1 = (bf16[3,128,128]{2,1,0:T(8,128)(2,1)S(1)}, bf16[3,128,128]{2,1,0:T(8,128)(2,1)S(1)}, u32[]{:S(2)}, u32[]{:S(2)}) collective-permute-start(bf16[3,128,128]{2,1,0:T(8,128)(2,1)S(1)} %get-tuple-element.41), channel_id=1, source_target_pairs={{0,2},{1,31},{2,4},{3,1},{4,6},{5,3},{6,8},{7,5},{8,10},{9,7},{10,... | collective-permute-start | bytes 294920 | tf_op jit(solution)/shard_map/ppermute | solution.py:521
  4.9 7.7 %collective-permute-start.2 = (bf16[3,128,128]{2,1,0:T(8,128)(2,1)S(1)}, bf16[3,128,128]{2,1,0:T(8,128)(2,1)S(1)}, u32[]{:S(2)}, u32[]{:S(2)}) collective-permute-start(bf16[3,128,128]{2,1,0:T(8,128)(2,1)S(1)} %get-tuple-element.42), channel_id=1, source_target_pairs={{0,31},{1,2},{2,1},{3,4},{4,3},{5,6},{6,5},{7,8},{8,7},{9,10},{10,... | collective-permute-start | bytes 294920 | tf_op jit(solution)/shard_map/ppermute | solution.py:521
  9.5 5.4 %collective-permute-start = (bf16[3,128,128]{2,1,0:T(8,128)(2,1)S(1)}, bf16[3,128,128]{2,1,0:T(8,128)(2,1)S(1)}, u32[]{:S(2)}, u32[]{:S(2)}) collective-permute-start(bf16[3,128,128]{2,1,0:T(8,128)(2,1)S(1)} %get-tuple-element.40), channel_id=1, source_target_pairs={{0,1},{1,0},{2,3},{3,2},{4,5},{5,4},{6,7},{7,6},{8,9},{9,8},{10,11... | collective-permute-start | bytes 294920 | tf_op jit(solution)/shard_map/ppermute | solution.py:521
  18.0 14.1 %all-to-all-start = ((bf16[32,24,128]{2,1,0:T(8,128)(2,1)}), bf16[32,24,128]{2,1,0:T(8,128)(2,1)S(1)}, u32[]{:S(2)}, u32[]{:S(2)}) async-start(bf16[32,24,128]{2,1,0:T(8,128)(2,1)} %get-tuple-element.59), calls=%async_computation | async-start | bytes 393216 | tf_op jit(solution)/shard_map/all_to_all | solution.py:668
  32.8 12.2 %all-to-all-start.1 = ((bf16[32,24,128]{2,1,0:T(8,128)(2,1)}), bf16[32,24,128]{2,1,0:T(8,128)(2,1)S(1)}, u32[]{:S(2)}, u32[]{:S(2)}) async-start(bf16[32,24,128]{2,1,0:T(8,128)(2,1)} %shard_map.99), calls=%async_computation.1 | async-start | bytes 393216 | tf_op jit(solution)/shard_map/all_to_all | solution.py:695
  35.4 7.2 %collective-permute-start.4 = (bf16[4,128,128]{2,1,0:T(8,128)(2,1)S(1)}, bf16[4,128,128]{2,1,0:T(8,128)(2,1)S(1)}, u32[]{:S(2)}, u32[]{:S(2)}) collective-permute-start(bf16[4,128,128]{2,1,0:T(8,128)(2,1)S(1)} %get-tuple-element.66), channel_id=1, source_target_pairs={{0,1},{1,0},{2,3},{3,2},{4,5},{5,4},{6,7},{7,6},{8,9},{9,8},{10,11... | collective-permute-start | bytes 393224 | tf_op jit(solution)/shard_map/ppermute | solution.py:685

commit v3 on v2

--- a/solution.py
+++ b/solution.py
@@ -376,36 +376,54 @@
         [layer_shifts(own_half(gb[j, pl.ds(LAYERS + own_at_c, own_c), :wide], j)) for j in range(nc)], axis=0
     )
     rhs = jnp.concatenate([taps(cz, j + 1, own_at_c, own_c) for j in range(nc)], axis=0)
-    acc_b[...] = dot_rows(lhs, rhs)
+    acc_b[...] = dot_rows(rhs, lhs)
     lhs = jnp.concatenate([gat[j, pl.ds(own_at_c, own_c), :] for j in range(nc)], axis=0)
     rhs = jnp.concatenate([own_half(fold[j, pl.ds(own_at_c, own_c), :], j) for j in range(nc)], axis=0)
-    mixed = dot_rows(lhs, rhs)
-    mix_sum = mixed[:c2, :c1]
+    mixed = dot_rows(rhs, lhs)
+    mix_sum = mixed[:c1, :c2]
     for p in range(1, PB):
-        mix_sum = mix_sum + mixed[p * c2 : (p + 1) * c2, p * c1 : (p + 1) * c1]
-    packed[c1:, 27 * c1 : 28 * c1] = mix_sum
-    packed[:c1, 27 * c1 : 28 * c1] = jnp.zeros((c1, c1), F32)
+        mix_sum = mix_sum + mixed[p * c1 : (p + 1) * c1, p * c2 : (p + 1) * c2]
+    first_b, first_mix = places_of(c1, c2)
+    packed[:, first_mix : first_mix + c2] = mix_sum
+    packed[:, 27 * c1 : first_b] = jnp.zeros((c1, first_b - 27 * c1), F32)
     span = 2 * width
-    for acc, outs, first in ((acc_a, c1, 0), (acc_b, c2, c1)):
-        for b in range(3):
-            for c in range(3):
-                total = None
-                for p in range(PB):
-                    at = (c * PB + p) * outs
-                    part = acc[at : at + outs, b * span : (b + 1) * span]
-                    part = pltpu.roll(part, (span - (p - 1) * c1) % span, 1)
-                    total = part if total is None else total + part
-                for a in range(3):
-                    t = 9 * a + 3 * b + c
-                    packed[first : first + outs, t * c1 : (t + 1) * c1] = total[:, a * c1 : (a + 1) * c1]
-    chunk = pk_ref.shape[1]
-    per = packed.shape[0] // chunk
-    used = packed.shape[1] // 128 * per
-    for v in range(packed.shape[1] // 128):
-        for r in range(per):
-            pk_ref[v * per + r] = packed[r * chunk : (r + 1) * chunk, v * 128 : (v + 1) * 128].astype(BF)
-    for v in range(used, pk_ref.shape[0]):
-        pk_ref[v] = jnp.zeros(pk_ref.shape[1:], BF)
+    for b in range(3):
+        for c in range(3):
+            total = None
+            for p in range(PB):
+                at = (c * PB + p) * c1
+                part = acc_a[at : at + c1, b * span : (b + 1) * span]
+                part = pltpu.roll(part, (span - (p - 1) * c1) % span, 1)
+                total = part if total is None else total + part
+            for a in range(3):
+                t = 9 * a + 3 * b + c
+                packed[:, t * c1 : (t + 1) * c1] = total[:, a * c1 : (a + 1) * c1]
+    for t in range(27):
+        a, b, c = t // 9, t // 3 % 3, t % 3
+        sides = [None, None]
+        for p in range(PB):
+            at = b * span + (p + a - 1) % (2 * PB) * c1
+            lanes = c * wide + p // 2 * 2 * c2
+            part = acc_b[at : at + c1, lanes : lanes + 2 * c2]
+            sides[p % 2] = part if sides[p % 2] is None else sides[p % 2] + part
+        total = sides[t % 2] + pltpu.roll(sides[1 - t % 2], c2, 1)
+        lanes = first_b + t * c2
+        packed[:, lanes : lanes + c2] = total[:, t % 2 * c2 : (t % 2 + 1) * c2]
+    step = pk_ref.shape[1] // 8
+    pieces8 = packed.shape[0] // 8
+    used = packed.shape[1] // 128 * pieces8
+    for n in range(pk_ref.shape[0] * step):
+        at = slice(n % step * 8, n % step * 8 + 8)
+        if n < used:
+            v, k = n // pieces8, n % pieces8
+            pk_ref[n // step, at] = packed[8 * k : 8 * k + 8, v * 128 : (v + 1) * 128].astype(BF)
+        else:
+            pk_ref[n // step, at] = jnp.zeros((8, 128), BF)
+
+
+def places_of(c1, c2):
+    first_b = -(-27 * c1 // 128) * 128
+    return first_b, first_b + 27 * c2
 
 
 def finish_kernel(paired, *refs):
@@ -461,16 +479,18 @@
 
 
 def post_kernel(factor, x_ref, ga_ref, gb_ref, gm_ref, buf):
-    chunk = x_ref.shape[1]
-    per = buf.shape[0] // chunk
-    c1 = ga_ref.shape[1]
-    for v in range(buf.shape[1] // 128):
-        for r in range(per):
-            buf[r * chunk : (r + 1) * chunk, v * 128 : (v + 1) * 128] = x_ref[v * per + r].astype(F32) * factor
+    step = x_ref.shape[1] // 8
+    pieces8 = buf.shape[0] // 8
+    c1, c2 = gm_ref.shape
+    for n in range(buf.shape[1] // 128 * pieces8):
+        v, k = n // pieces8, n % pieces8
+        part = x_ref[n // step, n % step * 8 : n % step * 8 + 8]
+        buf[8 * k : 8 * k + 8, v * 128 : (v + 1) * 128] = part.astype(F32) * factor
+    first_b, first_mix = places_of(c1, c2)
     for t in range(27):
-        ga_ref[t] = buf[:c1, t * c1 : (t + 1) * c1]
-        gb_ref[t] = buf[c1:, t * c1 : (t + 1) * c1].T
-    gm_ref[...] = buf[c1:, 27 * c1 : 28 * c1].T
+        ga_ref[t] = buf[:, t * c1 : (t + 1) * c1]
+        gb_ref[t] = buf[:, first_b + t * c2 : first_b + (t + 1) * c2]
+    gm_ref[...] = buf[:, first_mix : first_mix + c2]
 
 
 def call(kernel, outs, *args, scratch=(), smem=0, near=(), far=(), aliases={}):
@@ -613,9 +633,8 @@
     nc = nbx // 2 - 1
     rows_c = rows // 2
     devices = lax.axis_size("phi") * n_eta
-    lanes = 28 * c1
-    total_rows = (c1 + c2) * lanes // 128
-    chunk = next(d for d in range(8, c1 + c2 + 1, 8) if (c1 + c2) % d == 0 and total_rows <= d * devices)
+    lanes = places_of(c1, c2)[1] + c2
+    chunk = 8 * -(-c1 * lanes // (8 * 128 * devices))
     tall = rows + 2 * LAYERS
     tall_c = rows_c + 2 * LAYERS
     skip = len(meta)
@@ -660,7 +679,7 @@
             pltpu.VMEM((nc, rows_c, width), BF),
             pltpu.VMEM((3 * width, 6 * width), F32),
             pltpu.VMEM((3 * PB * c2, 6 * width), F32),
-            pltpu.VMEM((c1 + c2, lanes), F32),
+            pltpu.VMEM((c1, lanes), F32),
         ),
         smem=skip,
         near=range(skip + 1, skip + count + len(inner)),
@@ -698,7 +717,7 @@
         functools.partial(post_kernel, 1.0 / math.sqrt(cell_count)),
         (shape((27, c1, c1), F32), shape((27, c1, c2), F32), shape((c1, c2), F32)),
         sums,
-        scratch=(pltpu.VMEM((c1 + c2, lanes), F32),),
+        scratch=(pltpu.VMEM((c1, lanes), F32),),
         near=(0,),
     )
     return output, grad_input, grad_a, jnp.swapaxes(grad_b, 1, 2), grad_mix

time: 46.7 us -> 46.2 us (0.989)
  Pallas kernels: 12.5 us -> 12 us
    pallas_call x9, Pallas kernels: 12.5 us -> 12 us  [call(): pl.pallas_call(kernel, out_shape=outs, in_specs=specs, out_specs=tuple((p...]
where the time goes in v3:
time: 46.2 us; the launch traced here: 45.9 us
  waiting for transfers between devices  16.7 us (36%)
  starting transfers between devices  16.5 us (36%)
  Pallas kernels  12 us (26%)
  between operations  0.7 us (2%)
    pallas_call x9, Pallas kernels, call(): pl.pallas_call(kernel, out_shape=outs, in_specs=specs, out_specs=tuple((p...  12 us
    all_to_all x1, waiting for transfers between devices, shards(): terms = lax.all_to_all(terms, AXES, 0, 0, tiled=True)  8.89 us
    ppermute x4, starting transfers between devices, send(): return lax.ppermute(value, AXES, moves(n_phi, 2, rule))  7.65 us
    ppermute x1, waiting for transfers between devices, shards(): lax.ppermute(sent, AXES, moves(lax.axis_size('phi'), 2, lambda p, s: (0,...  5.46 us
    all_to_all x1, starting transfers between devices, shards(): terms = lax.all_to_all(terms, AXES, 0, 0, tiled=True)  4.51 us
    all_to_all x1, starting transfers between devices, shards(): sums = lax.all_to_all(sums, AXES, 0, 0, tiled=True)  2.58 us
    ppermute x1, starting transfers between devices, shards(): lax.ppermute(sent, AXES, moves(lax.axis_size('phi'), 2, lambda p, s: (0,...  1.72 us
    all_to_all x1, waiting for transfers between devices, shards(): sums = lax.all_to_all(sums, AXES, 0, 0, tiled=True)  1.66 us
  transfers between devices with their start and end apart: 7, of which 5 were waited for; matrix products, arithmetic and copies ran while one was open for 0% of the time, Pallas kernels for 13%

profile of v3, /device:TPU:0, one launch (start us, length us, event | category | flops | bytes accessed | tf_op | source)
XLA Modules:
  0.0 45.9 jit_solution(6727422471213852492)
XLA Ops:
  0.6 1.2 %shard_map.92 = (bf16[4,128,128]{2,1,0:T(8,128)(2,1)S(1)}, bf16[4,128,128]{2,1,0:T(8,128)(2,1)S(1)}, bf16[3,128,128]{2,1,0:T(8,128)(2,1)S(1)}, bf16[3,128,128]{2,1,0:T(8,128)(2,1)S(1)}, bf16[3,128,128]{2,1,0:T(8,128)(2,1)S(1)}) custom-call(bf16[32,16,128]{2,1,0:T(8,128)(2,1)} %f_hbm.1, bf16[32,16,128]{2,1,0:T(8,128)(2,1)} %c_hbm.1), custom_call_target="tpu_custom_call" | custom-call | tf_op jit(solution)/shard_map/pallas_call | solution.py:509
  1.9 3.1 %collective-permute-start.3 = (bf16[4,128,128]{2,1,0:T(8,128)(2,1)S(1)}, bf16[4,128,128]{2,1,0:T(8,128)(2,1)S(1)}, u32[]{:S(2)}, u32[]{:S(2)}) collective-permute-start(bf16[4,128,128]{2,1,0:T(8,128)(2,1)S(1)} %get-tuple-element.43.own), channel_id=1, source_target_pairs={{0,1},{1,0},{2,3},{3,2},{4,5},{5,4},{6,7},{7,6},{8,9},{9,8},{10,11... | collective-permute-start | bytes 393224 | tf_op jit(solution)/shard_map/ppermute | solution.py:541
  4.9 0.0 collective-permute-start.1
  4.9 4.6 %collective-permute-start.2 = (bf16[3,128,128]{2,1,0:T(8,128)(2,1)S(1)}, bf16[3,128,128]{2,1,0:T(8,128)(2,1)S(1)}, u32[]{:S(2)}, u32[]{:S(2)}) collective-permute-start(bf16[3,128,128]{2,1,0:T(8,128)(2,1)S(1)} %get-tuple-element.42), channel_id=1, source_target_pairs={{0,31},{1,2},{2,1},{3,4},{4,3},{5,6},{6,5},{7,8},{8,7},{9,10},{10,... | collective-permute-start | bytes 294920 | tf_op jit(solution)/shard_map/ppermute | solution.py:541
  9.5 0.0 collective-permute-start
  9.5 2.0 %shard_map.93 = (bf16[768,384]{1,0:T(8,128)(2,1)S(1)}, bf16[768,384]{1,0:T(8,128)(2,1)S(1)}, bf16[768,768]{1,0:T(8,128)(2,1)S(1)}, bf16[1152,384]{1,0:T(8,128)(2...) custom-call(bf16[27,32,32]{2,1,0:T(8,128)(2,1)} %ka_hbm.1, ...), custom_call_target="tpu_custom_call" | custom-call | tf_op jit(solution)/shard_map/pallas_call | solution.py:509
  11.6 0.0 collective-permute-done.3.partner
  11.6 0.9 %shard_map.94 = (bf16[6,320,256]{2,1,0:T(8,128)(2,1)S(1)}, bf16[6,256,128]{2,1,0:T(8,128)(2,1)S(1)}, f32[6,256,128]{2,1,0:T(8,128)S(1)}) custom-call(bf16[4,128,128]{2,1,0:T(8,128)(2,1)S(1)} %get-tuple-element.43.own, bf16[4,128,128]{2,1,0:T(8,128)(2,1)S(1)} %collective-permute-done.3.partner, bf16[768,384]{1,0:T(8,128)(2,1)S(1)} %get-tuple-element.44.wa.refs_5_), custom_call_target="tpu_custom_call" | custom-call | tf_op jit(solution)/shard_map/pallas_call | solution.py:509
  12.4 0.0 collective-permute-done.1.refs_0_.refs_2_
  12.4 0.2 collective-permute-done.2.refs_1_.refs_3_
  12.7 1.7 %shard_map.95 = (bf16[6,320,256]{2,1,0:T(8,128)(2,1)S(1)}, bf16[6,256,128]{2,1,0:T(8,128)(2,1)S(1)}, f32[6,256,128]{2,1,0:T(8,128)S(1)}, bf16[4,192,256]{2,1,0:T...) custom-call(bf16[3,128,128]{2,1,0:T(8,128)(2,1)S(1)} %collective-per, ...), custom_call_target="tpu_custom_call", output_to_operand_aliasing={{0}: (2, {}), {1}: (3, {}), {2}: (4, {})} | custom-call | tf_op jit(solution)/shard_map/pallas_call | solution.py:509
  14.4 0.5 %collective-permute-done.refs_1_ = bf16[3,128,128]{2,1,0:T(8,128)(2,1)S(1)} collective-permute-done((bf16[3,128,128]{2,1,0:T(8,128)(2,1)S(1)}, bf16[3,128,128]{2,1,0:T(8,128)(2,1)S(1)}, u32[]{:S(2)}, u32[]{:S(2)}) %collective-permute-start) | collective-permute-done | bytes 98336 | tf_op jit(solution)/shard_map/ppermute | solution.py:541
  14.9 2.8 %shard_map.96 = (bf16[6,320,256]{2,1,0:T(8,128)(2,1)S(1)}, bf16[32,24,128]{2,1,0:T(8,128)(2,1)}) custom-call(bf16[4,128,128]{2,1,0:T(8,128)(2,1)S(1)} %get-tuple-element.39.refs_0_, bf16[3,128,128]{2,1,0:T(8,128)(2,1)S(1)} %collective-permute-done.refs_1_, bf16[3,128,128]{2,1,0:T(8,128)(2,1)S(1)} %collective-permute-done.1.refs_0_.refs_2_, ...), custom_call_target="tpu_custom_call" | custom-call | tf_op jit(solution)/shard_map/pallas_call | solution.py:509
  17.7 4.5 %all-to-all-start = ((bf16[32,24,128]{2,1,0:T(8,128)(2,1)}), bf16[32,24,128]{2,1,0:T(8,128)(2,1)S(1)}, u32[]{:S(2)}, u32[]{:S(2)}) async-start(bf16[32,24,128]{2,1,0:T(8,128)(2,1)} %get-tuple-element.59), calls=%async_computation | async-start | bytes 393216 | tf_op jit(solution)/shard_map/all_to_all | solution.py:687
  22.2 0.7 %shard_map.97 = (bf16[4,128,128]{2,1,0:T(8,128)(2,1)S(1)}, bf16[4,128,128]{2,1,0:T(8,128)(2,1)S(1)}) custom-call(bf16[6,320,256]{2,1,0:T(8,128)(2,1)S(1)} %get-tuple-element.60.refs_0_, bf16[6,256,128]{2,1,0:T(8,128)(2,1)S(1)} %get-tuple-element.61.refs_1_, bf16[2,128,128]{2,1,0:T(8,128)(2,1)S(1)} %get-tuple-element.62.refs_2_, ...), custom_call_target="tpu_custom_call" | custom-call | tf_op jit(solution)/shard_map/pallas_call | solution.py:509
  23.0 8.9 %all-to-all-done.x_ref = bf16[32,24,128]{2,1,0:T(8,128)(2,1)S(1)} async-done(((bf16[32,24,128]{2,1,0:T(8,128)(2,1)}), bf16[32,24,128]{2,1,0:T(8,128)(2,1)S(1)}, u32[]{:S(2)}, u32[]{:S(2)}) %all-to-all-start) | async-done | bytes 196640 | tf_op jit(solution)/shard_map/all_to_all | solution.py:687
  31.8 0.7 %shard_map.99 = bf16[32,24,128]{2,1,0:T(8,128)(2,1)} custom-call(bf16[32,24,128]{2,1,0:T(8,128)(2,1)S(1)} %all-to-all-done.x_ref), custom_call_target="tpu_custom_call" | custom-call | tf_op jit(solution)/shard_map/pallas_call | solution.py:509
  32.6 2.6 %all-to-all-start.1 = ((bf16[32,24,128]{2,1,0:T(8,128)(2,1)}), bf16[32,24,128]{2,1,0:T(8,128)(2,1)S(1)}, u32[]{:S(2)}, u32[]{:S(2)}) async-start(bf16[32,24,128]{2,1,0:T(8,128)(2,1)} %shard_map.99), calls=%async_computation.1 | async-start | bytes 393216 | tf_op jit(solution)/shard_map/all_to_all | solution.py:714
  35.2 1.7 %collective-permute-start.4 = (bf16[4,128,128]{2,1,0:T(8,128)(2,1)S(1)}, bf16[4,128,128]{2,1,0:T(8,128)(2,1)S(1)}, u32[]{:S(2)}, u32[]{:S(2)}) collective-permute-start(bf16[4,128,128]{2,1,0:T(8,128)(2,1)S(1)} %get-tuple-element.66), channel_id=1, source_target_pairs={{0,1},{1,0},{2,3},{3,2},{4,5},{5,4},{6,7},{7,6},{8,9},{9,8},{10,11... | collective-permute-start | bytes 393224 | tf_op jit(solution)/shard_map/ppermute | solution.py:704
  36.9 5.5 %collective-permute-done.4.received = bf16[4,128,128]{2,1,0:T(8,128)(2,1)S(1)} collective-permute-done((bf16[4,128,128]{2,1,0:T(8,128)(2,1)S(1)}, bf16[4,128,128]{2,1,0:T(8,128)(2,1)S(1)}, u32[]{:S(2)}, u32[]{:S(2)}) %collective-permute-start.4) | collective-permute-done | bytes 131104 | tf_op jit(solution)/shard_map/ppermute | solution.py:704
  42.3 0.8 %shard_map.98 = (bf16[32,16,128]{2,1,0:T(8,128)(2,1)}, bf16[32,16,128]{2,1,0:T(8,128)(2,1)}) custom-call(bf16[4,128,128]{2,1,0:T(8,128)(2,1)S(1)} %get-tuple-element.65.kept, bf16[4,128,128]{2,1,0:T(8,128)(2,1)S(1)} %collective-permute-done.4.received), custom_call_target="tpu_custom_call" | custom-call | tf_op jit(solution)/shard_map/pallas_call | solution.py:509
  43.1 1.7 %all-to-all-done.1.x_ref = bf16[32,24,128]{2,1,0:T(8,128)(2,1)S(1)} async-done(((bf16[32,24,128]{2,1,0:T(8,128)(2,1)}), bf16[32,24,128]{2,1,0:T(8,128)(2,1)S(1)}, u32[]{:S(2)}, u32[]{:S(2)}) %all-to-all-start.1) | async-done | bytes 196640 | tf_op jit(solution)/shard_map/all_to_all | solution.py:714
  44.8 1.1 %shard_map.100 = (f32[27,32,32]{2,1,0:T(8,128)}, f32[27,32,64]{2,1,0:T(8,128)}, f32[32,64]{1,0:T(8,128)}) custom-call(bf16[32,24,128]{2,1,0:T(8,128)(2,1)S(1)} %all-to-all-done.1.x_ref), custom_call_target="tpu_custom_call" | custom-call | tf_op jit(solution)/shard_map/pallas_call | solution.py:509
Async XLA Ops:
  1.9 9.7 %collective-permute-start.3 = (bf16[4,128,128]{2,1,0:T(8,128)(2,1)S(1)}, bf16[4,128,128]{2,1,0:T(8,128)(2,1)S(1)}, u32[]{:S(2)}, u32[]{:S(2)}) collective-permute-start(bf16[4,128,128]{2,1,0:T(8,128)(2,1)S(1)} %get-tuple-element.43.own), channel_id=1, source_target_pairs={{0,1},{1,0},{2,3},{3,2},{4,5},{5,4},{6,7},{7,6},{8,9},{9,8},{10,11... | collective-permute-start | bytes 393224 | tf_op jit(solution)/shard_map/ppermute | solution.py:541
  4.9 7.5 %collective-permute-start.1 = (bf16[3,128,128]{2,1,0:T(8,128)(2,1)S(1)}, bf16[3,128,128]{2,1,0:T(8,128)(2,1)S(1)}, u32[]{:S(2)}, u32[]{:S(2)}) collective-permute-start(bf16[3,128,128]{2,1,0:T(8,128)(2,1)S(1)} %get-tuple-element.41), channel_id=1, source_target_pairs={{0,2},{1,31},{2,4},{3,1},{4,6},{5,3},{6,8},{7,5},{8,10},{9,7},{10,... | collective-permute-start | bytes 294920 | tf_op jit(solution)/shard_map/ppermute | solution.py:541
  4.9 7.7 %collective-permute-start.2 = (bf16[3,128,128]{2,1,0:T(8,128)(2,1)S(1)}, bf16[3,128,128]{2,1,0:T(8,128)(2,1)S(1)}, u32[]{:S(2)}, u32[]{:S(2)}) collective-permute-start(bf16[3,128,128]{2,1,0:T(8,128)(2,1)S(1)} %get-tuple-element.42), channel_id=1, source_target_pairs={{0,31},{1,2},{2,1},{3,4},{4,3},{5,6},{6,5},{7,8},{8,7},{9,10},{10,... | collective-permute-start | bytes 294920 | tf_op jit(solution)/shard_map/ppermute | solution.py:541
  9.5 5.4 %collective-permute-start = (bf16[3,128,128]{2,1,0:T(8,128)(2,1)S(1)}, bf16[3,128,128]{2,1,0:T(8,128)(2,1)S(1)}, u32[]{:S(2)}, u32[]{:S(2)}) collective-permute-start(bf16[3,128,128]{2,1,0:T(8,128)(2,1)S(1)} %get-tuple-element.40), channel_id=1, source_target_pairs={{0,1},{1,0},{2,3},{3,2},{4,5},{5,4},{6,7},{7,6},{8,9},{9,8},{10,11... | collective-permute-start | bytes 294920 | tf_op jit(solution)/shard_map/ppermute | solution.py:541
  17.7 14.1 %all-to-all-start = ((bf16[32,24,128]{2,1,0:T(8,128)(2,1)}), bf16[32,24,128]{2,1,0:T(8,128)(2,1)S(1)}, u32[]{:S(2)}, u32[]{:S(2)}) async-start(bf16[32,24,128]{2,1,0:T(8,128)(2,1)} %get-tuple-element.59), calls=%async_computation | async-start | bytes 393216 | tf_op jit(solution)/shard_map/all_to_all | solution.py:687
  32.6 12.2 %all-to-all-start.1 = ((bf16[32,24,128]{2,1,0:T(8,128)(2,1)}), bf16[32,24,128]{2,1,0:T(8,128)(2,1)S(1)}, u32[]{:S(2)}, u32[]{:S(2)}) async-start(bf16[32,24,128]{2,1,0:T(8,128)(2,1)} %shard_map.99), calls=%async_computation.1 | async-start | bytes 393216 | tf_op jit(solution)/shard_map/all_to_all | solution.py:714
  35.2 7.2 %collective-permute-start.4 = (bf16[4,128,128]{2,1,0:T(8,128)(2,1)S(1)}, bf16[4,128,128]{2,1,0:T(8,128)(2,1)S(1)}, u32[]{:S(2)}, u32[]{:S(2)}) collective-permute-start(bf16[4,128,128]{2,1,0:T(8,128)(2,1)S(1)} %get-tuple-element.66), channel_id=1, source_target_pairs={{0,1},{1,0},{2,3},{3,2},{4,5},{5,4},{6,7},{7,6},{8,9},{9,8},{10,11... | collective-permute-start | bytes 393224 | tf_op jit(solution)/shard_map/ppermute | solution.py:704

commit v4 on v3

--- a/solution.py
+++ b/solution.py
@@ -43,7 +43,7 @@
         ch, _, cells = ref.shape
         swapped = jnp.swapaxes(ref[...].astype(F32), 0, 1)
         for j in range(nb):
-            own[j] = swapped[PB * j : PB * (j + 1)].reshape(PB * ch, cells).T.astype(BF)
+            own[j] = swapped[PB * j : PB * (j + 1)].reshape(PB * ch, cells).astype(BF).T
     e = lax.axis_index("eta") if paired else 1
     for rim, low in ((first, e), (second, 1 - e)):
         for j in range(2):
@@ -249,8 +249,8 @@
     pieces, refs = refs[:count], refs[count:]
     if paired:
         refs = refs[3:]
-    wa, wb, mp, pool = refs[:4]
-    fz, hid, slope, cz, gat, slope_b, proj, half_way = refs[4:]
+    wa, wb, pool = refs[:3]
+    fz, hid, slope, cz, gat, slope_b, half_way = refs[3:]
     nbx = fz.shape[0]
     nc = gat.shape[0]
     rows = hid.shape[1]
@@ -295,7 +295,6 @@
         gated = (linear * logistic).astype(BF)
         gat[j] = gated
         slope_b[j] = logistic * (1.0 + linear * (1.0 - logistic))
-        proj[j] = dot(gated, mp[...]).astype(BF)
 
 
 def backward_kernel(paired, count, *refs):
@@ -430,8 +429,8 @@
     meta = None
     if not paired:
         meta, refs = refs[0], refs[1:]
-    gz, hid, proj, waf, up = refs[:5]
-    outs = refs[5:-1]
+    gz, hid, gat, waf, mp, up = refs[:6]
+    outs = refs[6:-1]
     buf = refs[-1]
     nb = gz.shape[0] - 4
     width = hid.shape[2]
@@ -456,7 +455,8 @@
         write(grad, nb + j)
     for j in range(nb):
         k = (j + 1) % 2
-        spread = dot(proj[(j + 1) // 2, pl.ds(own_at_c, own // 2), :], up[:, k * width : (k + 1) * width])
+        projected = dot(gat[(j + 1) // 2, pl.ds(own_at_c, own // 2), :], mp[...]).astype(BF)
+        spread = dot(projected, up[:, k * width : (k + 1) * width])
         write(hid[2 + j, pl.ds(own_at, own), :].astype(F32) + widen_rows(spread), j)
 
 
@@ -639,7 +639,7 @@
     tall_c = rows_c + 2 * LAYERS
     skip = len(meta)
     count = len(f_pieces)
-    matrices = (wa, wb, mp, pool)
+    matrices = (wa, wb, pool)
     fine = (
         pltpu.VMEM((nbx, tall, 2 * width), BF),
         pltpu.VMEM((nbx, rows, width), BF),
@@ -649,7 +649,6 @@
         pltpu.VMEM((nc + 2, tall_c, 2 * width), BF),
         pltpu.VMEM((nc, rows_c, PB * c2), BF),
         pltpu.VMEM((nc, rows_c, PB * c2), F32),
-        pltpu.VMEM((nc, rows_c, width), BF),
     )
     between = lambda n: (pltpu.VMEM((n, tall, 2 * width), BF),)
     if paired:
@@ -659,7 +658,7 @@
     else:
         args = (*meta, *f_pieces, *matrices)
         extra = {"near": range(skip + 1, len(args)), "smem": skip}
-    fz, hid, slope, cz, gat, slope_b, proj = call(
+    fz, hid, slope, cz, gat, slope_b = call(
         functools.partial(forward_kernel, paired, 2 if paired else count),
         fine + pooled,
         *args,
@@ -692,12 +691,13 @@
         *meta,
         gz,
         hid,
-        proj,
+        gat,
         waf,
+        mp,
         up,
         scratch=(pltpu.VMEM((blocks, rows if paired else cells, width), F32),),
         smem=skip,
-        near=range(skip, skip + 5),
+        near=range(skip, skip + 6),
     )
     if paired:
         kept, sent = results

time: 46.2 us -> 45.7 us (0.989)
  no operation moved by 1% of the time
where the time goes in v4:
time: 45.7 us; the launch traced here: 45.5 us
  waiting for transfers between devices  16.9 us (37%)
  starting transfers between devices  16.1 us (35%)
  Pallas kernels  11.8 us (26%)
  between operations  0.71 us (2%)
    pallas_call x9, Pallas kernels, call(): pl.pallas_call(kernel, out_shape=outs, in_specs=specs, out_specs=tuple((p...  11.8 us
    all_to_all x1, waiting for transfers between devices, shards(): terms = lax.all_to_all(terms, AXES, 0, 0, tiled=True)  8.67 us
    ppermute x4, starting transfers between devices, send(): return lax.ppermute(value, AXES, moves(n_phi, 2, rule))  7.65 us
    ppermute x1, waiting for transfers between devices, shards(): lax.ppermute(sent, AXES, moves(lax.axis_size('phi'), 2, lambda p, s: (0,...  5.46 us
    all_to_all x1, starting transfers between devices, shards(): terms = lax.all_to_all(terms, AXES, 0, 0, tiled=True)  4.11 us
    all_to_all x1, starting transfers between devices, shards(): sums = lax.all_to_all(sums, AXES, 0, 0, tiled=True)  2.58 us
    ppermute x1, starting transfers between devices, shards(): lax.ppermute(sent, AXES, moves(lax.axis_size('phi'), 2, lambda p, s: (0,...  1.72 us
    all_to_all x1, waiting for transfers between devices, shards(): sums = lax.all_to_all(sums, AXES, 0, 0, tiled=True)  1.66 us
  transfers between devices with their start and end apart: 7, of which 5 were waited for; matrix products, arithmetic and copies ran while one was open for 0% of the time, Pallas kernels for 13%

profile of v4, /device:TPU:0, one launch (start us, length us, event | category | flops | bytes accessed | tf_op | source)
XLA Modules:
  0.0 45.5 jit_solution(917614889891992970)
XLA Ops:
  0.6 1.2 %shard_map.92 = (bf16[4,128,128]{2,1,0:T(8,128)(2,1)S(1)}, bf16[4,128,128]{2,1,0:T(8,128)(2,1)S(1)}, bf16[3,128,128]{2,1,0:T(8,128)(2,1)S(1)}, bf16[3,128,128]{2,1,0:T(8,128)(2,1)S(1)}, bf16[3,128,128]{2,1,0:T(8,128)(2,1)S(1)}) custom-call(bf16[32,16,128]{2,1,0:T(8,128)(2,1)} %f_hbm.1, bf16[32,16,128]{2,1,0:T(8,128)(2,1)} %c_hbm.1), custom_call_target="tpu_custom_call" | custom-call | tf_op jit(solution)/shard_map/pallas_call | solution.py:509
  1.8 3.1 %collective-permute-start.3 = (bf16[4,128,128]{2,1,0:T(8,128)(2,1)S(1)}, bf16[4,128,128]{2,1,0:T(8,128)(2,1)S(1)}, u32[]{:S(2)}, u32[]{:S(2)}) collective-permute-start(bf16[4,128,128]{2,1,0:T(8,128)(2,1)S(1)} %get-tuple-element.42.own), channel_id=1, source_target_pairs={{0,1},{1,0},{2,3},{3,2},{4,5},{5,4},{6,7},{7,6},{8,9},{9,8},{10,11... | collective-permute-start | bytes 393224 | tf_op jit(solution)/shard_map/ppermute | solution.py:541
  4.9 0.0 collective-permute-start.1
  4.9 4.6 %collective-permute-start.2 = (bf16[3,128,128]{2,1,0:T(8,128)(2,1)S(1)}, bf16[3,128,128]{2,1,0:T(8,128)(2,1)S(1)}, u32[]{:S(2)}, u32[]{:S(2)}) collective-permute-start(bf16[3,128,128]{2,1,0:T(8,128)(2,1)S(1)} %get-tuple-element.41), channel_id=1, source_target_pairs={{0,31},{1,2},{2,1},{3,4},{4,3},{5,6},{6,5},{7,8},{8,7},{9,10},{10,... | collective-permute-start | bytes 294920 | tf_op jit(solution)/shard_map/ppermute | solution.py:541
  9.5 0.0 collective-permute-start
  9.5 2.0 %shard_map.93 = (bf16[768,384]{1,0:T(8,128)(2,1)S(1)}, bf16[768,384]{1,0:T(8,128)(2,1)S(1)}, bf16[768,768]{1,0:T(8,128)(2,1)S(1)}, bf16[1152,384]{1,0:T(8,128)(2...) custom-call(bf16[27,32,32]{2,1,0:T(8,128)(2,1)} %ka_hbm.1, ...), custom_call_target="tpu_custom_call" | custom-call | tf_op jit(solution)/shard_map/pallas_call | solution.py:509
  11.5 0.0 collective-permute-done.3.partner
  11.5 0.9 %shard_map.94 = (bf16[6,320,256]{2,1,0:T(8,128)(2,1)S(1)}, bf16[6,256,128]{2,1,0:T(8,128)(2,1)S(1)}, f32[6,256,128]{2,1,0:T(8,128)S(1)}) custom-call(bf16[4,128,128]{2,1,0:T(8,128)(2,1)S(1)} %get-tuple-element.42.own, bf16[4,128,128]{2,1,0:T(8,128)(2,1)S(1)} %collective-permute-done.3.partner, bf16[768,384]{1,0:T(8,128)(2,1)S(1)} %get-tuple-element.43.wa.refs_5_), custom_call_target="tpu_custom_call" | custom-call | tf_op jit(solution)/shard_map/pallas_call | solution.py:509
  12.4 0.0 collective-permute-done.1.refs_0_.refs_2_
  12.4 0.2 collective-permute-done.2.refs_1_.refs_3_
  12.6 1.4 %shard_map.95 = (bf16[6,320,256]{2,1,0:T(8,128)(2,1)S(1)}, bf16[6,256,128]{2,1,0:T(8,128)(2,1)S(1)}, f32[6,256,128]{2,1,0:T(8,128)S(1)}, bf16[4,192,256]{2,1,0:T...) custom-call(bf16[3,128,128]{2,1,0:T(8,128)(2,1)S(1)} %collective-per, ...), custom_call_target="tpu_custom_call", output_to_operand_aliasing={{0}: (2, {}), {1}: (3, {}), {2}: (4, {})} | custom-call | tf_op jit(solution)/shard_map/pallas_call | solution.py:509
  14.0 0.8 %collective-permute-done.refs_1_ = bf16[3,128,128]{2,1,0:T(8,128)(2,1)S(1)} collective-permute-done((bf16[3,128,128]{2,1,0:T(8,128)(2,1)S(1)}, bf16[3,128,128]{2,1,0:T(8,128)(2,1)S(1)}, u32[]{:S(2)}, u32[]{:S(2)}) %collective-permute-start) | collective-permute-done | bytes 98336 | tf_op jit(solution)/shard_map/ppermute | solution.py:541
  14.8 2.8 %shard_map.96 = (bf16[6,320,256]{2,1,0:T(8,128)(2,1)S(1)}, bf16[32,24,128]{2,1,0:T(8,128)(2,1)}) custom-call(bf16[4,128,128]{2,1,0:T(8,128)(2,1)S(1)} %get-tuple-element.38.refs_0_, bf16[3,128,128]{2,1,0:T(8,128)(2,1)S(1)} %collective-permute-done.refs_1_, bf16[3,128,128]{2,1,0:T(8,128)(2,1)S(1)} %collective-permute-done.1.refs_0_.refs_2_, ...), custom_call_target="tpu_custom_call" | custom-call | tf_op jit(solution)/shard_map/pallas_call | solution.py:509
  17.6 4.1 %all-to-all-start = ((bf16[32,24,128]{2,1,0:T(8,128)(2,1)}), bf16[32,24,128]{2,1,0:T(8,128)(2,1)S(1)}, u32[]{:S(2)}, u32[]{:S(2)}) async-start(bf16[32,24,128]{2,1,0:T(8,128)(2,1)} %get-tuple-element.57), calls=%async_computation | async-start | bytes 393216 | tf_op jit(solution)/shard_map/all_to_all | solution.py:686
  21.8 1.0 %shard_map.97 = (bf16[4,128,128]{2,1,0:T(8,128)(2,1)S(1)}, bf16[4,128,128]{2,1,0:T(8,128)(2,1)S(1)}) custom-call(bf16[6,320,256]{2,1,0:T(8,128)(2,1)S(1)} %get-tuple-element.58.refs_0_, bf16[6,256,128]{2,1,0:T(8,128)(2,1)S(1)} %get-tuple-element.59.refs_1_, bf16[2,128,256]{2,1,0:T(8,128)(2,1)S(1)} %get-tuple-element.52.refs_7_.refs_2_, ...), custom_call_target="tpu_custom_call" | custom-call | tf_op jit(solution)/shard_map/pallas_call | solution.py:509
  22.7 8.7 %all-to-all-done.x_ref = bf16[32,24,128]{2,1,0:T(8,128)(2,1)S(1)} async-done(((bf16[32,24,128]{2,1,0:T(8,128)(2,1)}), bf16[32,24,128]{2,1,0:T(8,128)(2,1)S(1)}, u32[]{:S(2)}, u32[]{:S(2)}) %all-to-all-start) | async-done | bytes 196640 | tf_op jit(solution)/shard_map/all_to_all | solution.py:686
  31.4 0.7 %shard_map.99 = bf16[32,24,128]{2,1,0:T(8,128)(2,1)} custom-call(bf16[32,24,128]{2,1,0:T(8,128)(2,1)S(1)} %all-to-all-done.x_ref), custom_call_target="tpu_custom_call" | custom-call | tf_op jit(solution)/shard_map/pallas_call | solution.py:509
  32.1 2.6 %all-to-all-start.1 = ((bf16[32,24,128]{2,1,0:T(8,128)(2,1)}), bf16[32,24,128]{2,1,0:T(8,128)(2,1)S(1)}, u32[]{:S(2)}, u32[]{:S(2)}) async-start(bf16[32,24,128]{2,1,0:T(8,128)(2,1)} %shard_map.99), calls=%async_computation.1 | async-start | bytes 393216 | tf_op jit(solution)/shard_map/all_to_all | solution.py:714
  34.7 1.7 %collective-permute-start.4 = (bf16[4,128,128]{2,1,0:T(8,128)(2,1)S(1)}, bf16[4,128,128]{2,1,0:T(8,128)(2,1)S(1)}, u32[]{:S(2)}, u32[]{:S(2)}) collective-permute-start(bf16[4,128,128]{2,1,0:T(8,128)(2,1)S(1)} %get-tuple-element.64), channel_id=1, source_target_pairs={{0,1},{1,0},{2,3},{3,2},{4,5},{5,4},{6,7},{7,6},{8,9},{9,8},{10,11... | collective-permute-start | bytes 393224 | tf_op jit(solution)/shard_map/ppermute | solution.py:704
  36.4 5.5 %collective-permute-done.4.received = bf16[4,128,128]{2,1,0:T(8,128)(2,1)S(1)} collective-permute-done((bf16[4,128,128]{2,1,0:T(8,128)(2,1)S(1)}, bf16[4,128,128]{2,1,0:T(8,128)(2,1)S(1)}, u32[]{:S(2)}, u32[]{:S(2)}) %collective-permute-start.4) | collective-permute-done | bytes 131104 | tf_op jit(solution)/shard_map/ppermute | solution.py:704
  41.9 0.8 %shard_map.98 = (bf16[32,16,128]{2,1,0:T(8,128)(2,1)}, bf16[32,16,128]{2,1,0:T(8,128)(2,1)}) custom-call(bf16[4,128,128]{2,1,0:T(8,128)(2,1)S(1)} %get-tuple-element.63.kept, bf16[4,128,128]{2,1,0:T(8,128)(2,1)S(1)} %collective-permute-done.4.received), custom_call_target="tpu_custom_call" | custom-call | tf_op jit(solution)/shard_map/pallas_call | solution.py:509
  42.7 1.7 %all-to-all-done.1.x_ref = bf16[32,24,128]{2,1,0:T(8,128)(2,1)S(1)} async-done(((bf16[32,24,128]{2,1,0:T(8,128)(2,1)}), bf16[32,24,128]{2,1,0:T(8,128)(2,1)S(1)}, u32[]{:S(2)}, u32[]{:S(2)}) %all-to-all-start.1) | async-done | bytes 196640 | tf_op jit(solution)/shard_map/all_to_all | solution.py:714
  44.4 1.1 %shard_map.100 = (f32[27,32,32]{2,1,0:T(8,128)}, f32[27,32,64]{2,1,0:T(8,128)}, f32[32,64]{1,0:T(8,128)}) custom-call(bf16[32,24,128]{2,1,0:T(8,128)(2,1)S(1)} %all-to-all-done.1.x_ref), custom_call_target="tpu_custom_call" | custom-call | tf_op jit(solution)/shard_map/pallas_call | solution.py:509
Async XLA Ops:
  1.8 9.7 %collective-permute-start.3 = (bf16[4,128,128]{2,1,0:T(8,128)(2,1)S(1)}, bf16[4,128,128]{2,1,0:T(8,128)(2,1)S(1)}, u32[]{:S(2)}, u32[]{:S(2)}) collective-permute-start(bf16[4,128,128]{2,1,0:T(8,128)(2,1)S(1)} %get-tuple-element.42.own), channel_id=1, source_target_pairs={{0,1},{1,0},{2,3},{3,2},{4,5},{5,4},{6,7},{7,6},{8,9},{9,8},{10,11... | collective-permute-start | bytes 393224 | tf_op jit(solution)/shard_map/ppermute | solution.py:541
  4.9 7.5 %collective-permute-start.1 = (bf16[3,128,128]{2,1,0:T(8,128)(2,1)S(1)}, bf16[3,128,128]{2,1,0:T(8,128)(2,1)S(1)}, u32[]{:S(2)}, u32[]{:S(2)}) collective-permute-start(bf16[3,128,128]{2,1,0:T(8,128)(2,1)S(1)} %get-tuple-element.40), channel_id=1, source_target_pairs={{0,2},{1,31},{2,4},{3,1},{4,6},{5,3},{6,8},{7,5},{8,10},{9,7},{10,... | collective-permute-start | bytes 294920 | tf_op jit(solution)/shard_map/ppermute | solution.py:541
  4.9 7.7 %collective-permute-start.2 = (bf16[3,128,128]{2,1,0:T(8,128)(2,1)S(1)}, bf16[3,128,128]{2,1,0:T(8,128)(2,1)S(1)}, u32[]{:S(2)}, u32[]{:S(2)}) collective-permute-start(bf16[3,128,128]{2,1,0:T(8,128)(2,1)S(1)} %get-tuple-element.41), channel_id=1, source_target_pairs={{0,31},{1,2},{2,1},{3,4},{4,3},{5,6},{6,5},{7,8},{8,7},{9,10},{10,... | collective-permute-start | bytes 294920 | tf_op jit(solution)/shard_map/ppermute | solution.py:541
  9.5 5.4 %collective-permute-start = (bf16[3,128,128]{2,1,0:T(8,128)(2,1)S(1)}, bf16[3,128,128]{2,1,0:T(8,128)(2,1)S(1)}, u32[]{:S(2)}, u32[]{:S(2)}) collective-permute-start(bf16[3,128,128]{2,1,0:T(8,128)(2,1)S(1)} %get-tuple-element.39), channel_id=1, source_target_pairs={{0,1},{1,0},{2,3},{3,2},{4,5},{5,4},{6,7},{7,6},{8,9},{9,8},{10,11... | collective-permute-start | bytes 294920 | tf_op jit(solution)/shard_map/ppermute | solution.py:541
  17.6 13.8 %all-to-all-start = ((bf16[32,24,128]{2,1,0:T(8,128)(2,1)}), bf16[32,24,128]{2,1,0:T(8,128)(2,1)S(1)}, u32[]{:S(2)}, u32[]{:S(2)}) async-start(bf16[32,24,128]{2,1,0:T(8,128)(2,1)} %get-tuple-element.57), calls=%async_computation | async-start | bytes 393216 | tf_op jit(solution)/shard_map/all_to_all | solution.py:686
  32.1 12.2 %all-to-all-start.1 = ((bf16[32,24,128]{2,1,0:T(8,128)(2,1)}), bf16[32,24,128]{2,1,0:T(8,128)(2,1)S(1)}, u32[]{:S(2)}, u32[]{:S(2)}) async-start(bf16[32,24,128]{2,1,0:T(8,128)(2,1)} %shard_map.99), calls=%async_computation.1 | async-start | bytes 393216 | tf_op jit(solution)/shard_map/all_to_all | solution.py:714
  34.7 7.2 %collective-permute-start.4 = (bf16[4,128,128]{2,1,0:T(8,128)(2,1)S(1)}, bf16[4,128,128]{2,1,0:T(8,128)(2,1)S(1)}, u32[]{:S(2)}, u32[]{:S(2)}) collective-permute-start(bf16[4,128,128]{2,1,0:T(8,128)(2,1)S(1)} %get-tuple-element.64), channel_id=1, source_target_pairs={{0,1},{1,0},{2,3},{3,2},{4,5},{5,4},{6,7},{7,6},{8,9},{9,8},{10,11... | collective-permute-start | bytes 393224 | tf_op jit(solution)/shard_map/ppermute | solution.py:704
